TPU v7x, 32 devices: a whole 2x2x4 slice. The times are simulated.
32 devices in a mesh: tp: 8 (over z, y), ep: 4 (over x, core).
Axes of the slice: x: 2, y: 2, z: 4, core: 2. Of those that a mesh axis runs over, the one named last changes fastest.
Arguments:
- tokens: bfloat16 [16384, 512], P('ep')
- w_router: float32 [512, 32], replicated
- expert_idx: int32 [16384, 2], P('ep')
- slot_idx: int32 [16384, 2], P('ep')
- w_gelu: bfloat16 [32, 512, 1024], P('ep', None, 'tp')
- w_linear: bfloat16 [32, 512, 1024], P('ep', None, 'tp')
- w_out: bfloat16 [32, 1024, 512], P('ep', 'tp')
- dy_tokens: bfloat16 [16384, 512], P('ep')
Outputs:
- output 1: bfloat16 [16384, 512], P('ep')
- output 2: bfloat16 [16384, 512], P('ep')
- output 3: bfloat16 [32, 512, 1024], P('ep', None, 'tp')
- output 4: bfloat16 [32, 512, 1024], P('ep', None, 'tp')
- output 5: bfloat16 [32, 1024, 512], P('ep', 'tp')
- output 6: float32 [512, 32], replicated
- output 7: float32 [], replicated
All inputs are finite; a program needn't handle non-finite values.
Results may differ from a plain program's by a relative error of at most 0.0160283.
Values are sent between devices in bfloat16 or wider.
A program may use at most 1 GiB of HBM per device.

v0:
```python
import jax
import jax.numpy as jnp
from jax import lax
from jax.sharding import PartitionSpec as P

AUX_WEIGHT = 0.01


def gated_gelu(pre_gelu, pre_lin):
    return jax.nn.gelu(pre_gelu, approximate=True) * pre_lin


def solution(mesh):
    ep_size = mesh.shape["ep"]
    tp_size = mesh.shape["tp"]

    def device_step(x_loc, w_router, idx_loc, slot_loc, gelu_loc, lin_loc, out_loc, dy_loc):
        shard_tokens, d_model = x_loc.shape
        exp_local = gelu_loc.shape[0]
        experts = exp_local * ep_size
        capacity = 4 * shard_tokens // experts
        slots_total = experts * capacity
        token_count = float(shard_tokens * ep_size)
        col_width = d_model // tp_size
        col_start = lax.axis_index("tp") * col_width
        choice_mask = idx_loc[:, :, None] == jnp.arange(experts)

        def router_fn(x_wide, router):
            logits = jnp.dot(x_wide, router, precision=lax.Precision.HIGHEST)
            prob_rows = jax.nn.softmax(logits, axis=-1)
            picked = jnp.sum(jnp.where(choice_mask, prob_rows[:, None, :], 0.0), axis=-1)
            return picked / jnp.sum(picked, axis=1, keepdims=True), jnp.sum(prob_rows, axis=0)

        (gate_vals, prob_sum), router_pull = jax.vjp(router_fn, x_loc.astype(jnp.float32), w_router)
        top_count = jnp.sum(choice_mask[:, 0, :], axis=0).astype(jnp.float32)
        route_stats = lax.psum(jnp.stack([top_count, prob_sum]), "ep")
        aux_loss = experts * jnp.sum(route_stats[0] * route_stats[1]) / (token_count * token_count)

        flat_pos = jnp.where(slot_loc < capacity, idx_loc * capacity + slot_loc, slots_total)
        choice_ids = jnp.full((slots_total,), 2 * shard_tokens, jnp.int32).at[flat_pos.reshape(-1)].set(jnp.arange(2 * shard_tokens, dtype=jnp.int32), mode="drop")
        token_ids = choice_ids // 2
        send_rows = jnp.take(x_loc, token_ids, axis=0, mode="fill", fill_value=0)
        recv_rows = lax.all_to_all(send_rows.reshape(ep_size, exp_local, capacity, d_model), "ep", 0, 0, tiled=True)

        pre_gelu = jnp.einsum("secd,edf->secf", recv_rows, gelu_loc, preferred_element_type=jnp.float32)
        pre_lin = jnp.einsum("secd,edf->secf", recv_rows, lin_loc, preferred_element_type=jnp.float32)
        hidden_wide, gelu_pull = jax.vjp(gated_gelu, pre_gelu, pre_lin)
        hidden = hidden_wide.astype(jnp.bfloat16)
        out_part = jnp.einsum("secf,efd->secd", hidden, out_loc, preferred_element_type=jnp.float32).astype(jnp.bfloat16)
        out_cols = lax.psum_scatter(out_part, "tp", scatter_dimension=3, tiled=True)
        back_cols = lax.all_to_all(out_cols, "ep", 0, 0, tiled=True).reshape(slots_total, col_width)
        chosen = jnp.take(back_cols, flat_pos, axis=0, mode="fill", fill_value=0)
        y_cols = (gate_vals[:, 0, None] * chosen[:, 0] + gate_vals[:, 1, None] * chosen[:, 1]).astype(jnp.bfloat16)
        y_loc = lax.all_gather(y_cols, "tp", axis=1, tiled=True)

        dy_cols = lax.dynamic_slice_in_dim(dy_loc, col_start, col_width, axis=1)
        gate_part = jnp.einsum("nd,nkd->nk", dy_cols, chosen, preferred_element_type=jnp.float32)
        d_gates = lax.psum(gate_part, "tp")
        gate_at_slot = jnp.take(gate_vals.reshape(-1), choice_ids, axis=0, mode="fill", fill_value=0)
        dy_at_slot = jnp.take(dy_cols, token_ids, axis=0, mode="fill", fill_value=0)
        d_back = (gate_at_slot[:, None] * dy_at_slot).astype(jnp.bfloat16)
        d_out_cols = lax.all_to_all(d_back.reshape(ep_size, exp_local, capacity, col_width), "ep", 0, 0, tiled=True)
        d_out = lax.all_gather(d_out_cols, "tp", axis=3, tiled=True)

        grad_out = jnp.einsum("secf,secd->efd", hidden, d_out, preferred_element_type=jnp.float32).astype(jnp.bfloat16)
        d_hidden = jnp.einsum("secd,efd->secf", d_out, out_loc, preferred_element_type=jnp.float32)
        d_pre_gelu, d_pre_lin = gelu_pull(d_hidden)
        d_pre_gelu = d_pre_gelu.astype(jnp.bfloat16)
        d_pre_lin = d_pre_lin.astype(jnp.bfloat16)
        grad_gelu = jnp.einsum("secd,secf->edf", recv_rows, d_pre_gelu, preferred_element_type=jnp.float32).astype(jnp.bfloat16)
        grad_lin = jnp.einsum("secd,secf->edf", recv_rows, d_pre_lin, preferred_element_type=jnp.float32).astype(jnp.bfloat16)
        d_recv = jnp.einsum("secf,edf->secd", d_pre_gelu, gelu_loc, preferred_element_type=jnp.float32)
        d_recv = (d_recv + jnp.einsum("secf,edf->secd", d_pre_lin, lin_loc, preferred_element_type=jnp.float32)).astype(jnp.bfloat16)
        d_recv_cols = lax.psum_scatter(d_recv, "tp", scatter_dimension=3, tiled=True)
        d_send = lax.all_to_all(d_recv_cols, "ep", 0, 0, tiled=True).reshape(slots_total, col_width)
        d_choice = jnp.take(d_send, flat_pos, axis=0, mode="fill", fill_value=0)
        d_tok_expert = jnp.sum(d_choice, axis=1, dtype=jnp.float32)

        aux_cot = AUX_WEIGHT * experts * route_stats[0] / (token_count * token_count)
        d_x_router, d_router_loc = router_pull((d_gates, aux_cot))
        grad_router = lax.psum(d_router_loc, "ep")
        dx_cols = (d_tok_expert + lax.dynamic_slice_in_dim(d_x_router, col_start, col_width, axis=1)).astype(jnp.bfloat16)
        dx_loc = lax.all_gather(dx_cols, "tp", axis=1, tiled=True)
        return y_loc, dx_loc, grad_gelu, grad_lin, grad_out, grad_router, aux_loss

    rows_spec = P("ep", None)
    weight_in = P("ep", None, "tp")
    weight_out = P("ep", "tp", None)
    mapped = jax.shard_map(
        device_step,
        mesh=mesh,
        in_specs=(rows_spec, P(None, None), rows_spec, rows_spec, weight_in, weight_in, weight_out, rows_spec),
        out_specs=(rows_spec, rows_spec, weight_in, weight_in, weight_out, P(None, None), P()),
        check_vma=False,
    )
    return mapped
```

profile of v0, /device:TPU:0, one launch (start us, length us, event | category | flops | bytes accessed | tf_op | source)
XLA Modules:
  0.0 1395.8 jit_solution(446027159899837205)
XLA Ops:
  7.2 1.5 compare_and_fusion
  8.8 0.6 copy-done.16
  9.4 0.6 copy.70
  10.0 1.4 reshape.133
  11.5 30.5 %scatter_custom_fusion = s32[16384]{0:T(1024)S(1)} fusion(s32[8192]{0:T(1024)S(1)} %bitcast.116, s32[8192]{0:T(1024)S(1)} %iota.7, s32[]{:T(128)} %constant.55.clone.1), kind=kCustom, calls=%fused_computation.89 | custom fusion | bytes 65540 | tf_op jit(solution)/shard_map/scatter | solution.py:40
  42.2 5.9 fusion.45
  48.2 0.7 copy-done.5
  48.9 0.7 fusion.42
  50.6 0.6 copy-done.18
  51.2 0.6 copy.80
  51.8 1.2 div.76
  53.1 90.5 %gather_fusion.1 = f32[16384]{0:T(1024)S(1)} fusion(f32[8192]{0:T(1024)S(1)} %div.76, s32[16384]{0:T(1024)S(1)} %get-tuple-element.47), kind=kCustom, calls=%fused_computation.3 | custom fusion | bytes 196608 | tf_op jit(solution)/shard_map/jit(_take)/gather | solution.py:59
  143.7 1.6 constant_dynamic-slice_fusion
  145.3 58.1 %gather_fusion.2 = bf16[16384,64]{1,0:T(8,128)(2,1)} fusion(bf16[4096,64]{1,0:T(8,128)(2,1)S(1)} %constant_dynamic-slice_fusion, s32[16384]{0:T(1024)S(1)} %get-tuple-element.48), kind=kCustom, calls=%fused_computation.4 | custom fusion | bytes 4259840 | tf_op jit(solution)/shard_map/jit(_take)/gather | solution.py:60
  203.3 4.7 copy.111
  208.6 1.2 copy.82
  209.7 29.8 %all_to_all.20 = bf16[4,8,512,64]{2,3,1,0:T(8,128)(2,1)S(1)} all-to-all(bf16[4,8,512,64]{2,3,1,0:T(8,128)(2,1)S(1)} %copy.82), channel_id=1, replica_groups=mesh['tp'=8,'ep'=4] {'ep'}, dimensions={0} | all-to-all | bytes 4194304 | tf_op jit(solution)/shard_map/all_to_all | solution.py:62
  239.5 1.5 copy.83
  241.4 69.6 %gather_fusion = bf16[16384,512]{1,0:T(8,128)(2,1)} fusion(bf16[4096,512]{1,0:T(8,128)(2,1)} %param.10, s32[16384]{0:T(1024)S(1)} %get-tuple-element.48), kind=kCustom, calls=%fused_computation.2 | custom fusion | bytes 33619968 | tf_op jit(solution)/shard_map/jit(_take)/gather | solution.py:42
  311.0 8.9 broadcast_select_fusion
  319.9 187.5 %all_to_all.21 = bf16[4,8,512,512]{3,2,1,0:T(8,128)(2,1)} all-to-all(bf16[4,8,512,512]{3,2,1,0:T(8,128)(2,1)S(1)} %broadcast_select_fusion), channel_id=1, replica_groups=mesh['tp'=8,'ep'=4] {'ep'}, dimensions={0} | all-to-all | bytes 33554432 | tf_op jit(solution)/shard_map/all_to_all | solution.py:43
  507.4 13.6 fusion.1
  521.0 13.5 fusion.3
  534.5 19.9 %fusion.12 = (bf16[4,8,512,128]{3,2,0,1:T(8,128)(2,1)}, bf16[4,8,512,128]{3,2,0,1:T(8,128)(2,1)}, bf16[4,8,512,128]{3,2,0,1:T(8,128)(2,1)}) fusion(f32[8,4,512,128]{3,2,1,0:T(8,128)} %fusion.3, f32[8,4,512,128]{3,2,1,0:T(8,128)} %fusion.1, bf16[4,8,512,512]{2,3,0,1:T(8,128)(2,1)} %all-gather.6.cloned.1.call-done, bf16[8,128,512]{2,1,0:T(8,128)(2,1)S(1)} %copy-done), kind=kOutput, calls=%fused_computation.25 | convolution fusion | flops 2202009600 | bytes 47185920 | tf_op jit(solution)/shard_map/secd,efd->secf/dot_general | solution.py:66
  554.4 20.5 %convert_bitcast_fusion = bf16[4,8,512,512]{3,2,0,1:T(8,128)(2,1)} fusion(bf16[4,8,512,128]{3,2,0,1:T(8,128)(2,1)} %get-tuple-element.46, bf16[8,128,512]{2,1,0:T(8,128)(2,1)S(1)} %copy-done), kind=kOutput, calls=%fused_computation.8 | convolution fusion | flops 2155872256 | bytes 22020096 | tf_op jit(solution)/shard_map/secf,efd->secd/dot_general | solution.py:49
  574.9 28.6 %copy.73 = bf16[4,8,512,512]{2,1,0,3:T(8,128)(2,1)} copy(bf16[4,8,512,512]{3,2,0,1:T(8,128)(2,1)} %convert_bitcast_fusion) | data formatting | bytes 33554432 | tf_op jit(solution)/shard_map/convert_element_type | solution.py:49
  603.6 15.5 %fusion.28 = f32[8,4,512,512]{3,2,1,0:T(8,128)} fusion(bf16[4,8,512,128]{3,2,0,1:T(8,128)(2,1)} %get-tuple-element.45, bf16[8,512,128]{2,1,0:T(8,128)(2,1)S(1)} %copy-done.9), kind=kOutput, calls=%fused_computation.52 | convolution fusion | flops 2147483648 | bytes 38797312 | tf_op jit(solution)/shard_map/secf,edf->secd/dot_general | solution.py:72
  619.1 18.4 %fusion = bf16[4,8,512,512]{3,2,0,1:T(8,128)(2,1)} fusion(f32[8,4,512,512]{3,2,1,0:T(8,128)} %fusion.28, bf16[4,8,512,128]{3,2,0,1:T(8,128)(2,1)} %get-tuple-element.44, bf16[8,512,128]{2,1,0:T(8,128)(2,1)S(1)} %copy-done.8), kind=kOutput, calls=%fused_computation.7 | convolution fusion | flops 2164260864 | bytes 55574528 | tf_op jit(solution)/shard_map/secf,edf->secd/dot_general | solution.py:73
  637.4 28.6 %copy.84 = bf16[4,8,512,512]{2,1,0,3:T(8,128)(2,1)} copy(bf16[4,8,512,512]{3,2,0,1:T(8,128)(2,1)} %fusion) | data formatting | bytes 33554432 | tf_op jit(solution)/shard_map/convert_element_type | solution.py:73
  666.1 1.2 copy-done.4
  667.3 1.3 copy.115
  668.6 214.0 %reduce-scatter.3.cloned.1.call-done = bf16[4,8,512,64]{2,1,0,3:T(8,128)(2,1)} async-done(((bf16[4,8,512,512]{2,1,0,3:T(8,128)(2,1)}), bf16[4,8,512,64]{2,1,0,3:T(8,128)(2,1)}) %reduce-scatter.3.cloned.1.call-update) | async-done | bytes 2097168 | tf_op jit(solution)/shard_map/reduce_scatter | solution.py:50
  882.6 4.1 copy.74
  886.7 3.7 all-to-all-start.1
  890.5 2.0 copy.76
  892.5 2.7 reshape.193
  895.3 20.6 %all-to-all-done.1 = bf16[4,8,512,64]{2,3,1,0:T(8,128)(2,1)S(1)} async-done(((bf16[4,8,512,64]{2,3,1,0:T(8,128)(2,1)}), bf16[4,8,512,64]{2,3,1,0:T(8,128)(2,1)S(1)}, u32[]{:S(2)}, u32[]{:S(2)}) %all-to-all-start.1) | async-done | bytes 2097184 | tf_op jit(solution)/shard_map/all_to_all | solution.py:51
  915.9 3.2 copy.110
  919.1 24.6 %gather_fusion.3 = bf16[8192,64]{1,0:T(8,128)(2,1)S(1)} fusion(bf16[16384,64]{1,0:T(8,128)(2,1)} %bitcast.109, s32[8192]{0:T(1024)S(1)} %broadcast_clamp_fusion.1), kind=kCustom, calls=%fused_computation.clone | custom fusion | bytes 2129920 | tf_op jit(solution)/shard_map/jit(_take)/gather | solution.py:52
  943.7 3.8 copy.78
  947.6 1.9 multiply_reduce_fusion
  949.5 1.0 fusion.25
  950.9 6.1 psum.21
  957.1 207.4 %reduce-scatter.5.cloned.1.call-done = bf16[4,8,512,64]{2,1,0,3:T(8,128)(2,1)} async-done(((bf16[4,8,512,512]{2,1,0,3:T(8,128)(2,1)}), bf16[4,8,512,64]{2,1,0,3:T(8,128)(2,1)}) %reduce-scatter.5.cloned.1.call-update) | async-done | bytes 2097168 | tf_op jit(solution)/shard_map/reduce_scatter | solution.py:74
  1164.5 4.1 copy.85
  1168.6 4.5 all-to-all-start.3
  1173.1 0.6 multiply_reduce_fusion.3
  1173.7 0.8 copy.79
  1174.6 36.6 %psum.22 = f32[4096,2]{0,1:T(2,128)S(1)} all-reduce(f32[4096,2]{0,1:T(2,128)S(1)} %get-tuple-element.40), channel_id=1, replica_groups=mesh['tp'=8,'ep'=4] {'tp'}, use_global_device_ids=true, to_apply=%region_11.13 | all-reduce | flops 8192 | bytes 65536 | tf_op jit(solution)/shard_map/psum | solution.py:58
  1211.7 4.8 copy.112
  1216.5 30.9 %gather_fusion.4 = bf16[8192,64]{1,0:T(8,128)(2,1)} fusion(bf16[16384,64]{1,0:T(8,128)(2,1)} %bitcast.108, s32[8192]{0:T(1024)S(1)} %broadcast_clamp_fusion.1), kind=kCustom, calls=%fused_computation.1.clone | custom fusion | bytes 2129920 | tf_op jit(solution)/shard_map/jit(_take)/gather | solution.py:76
  1247.4 25.2 %convert_reduce_fusion = f32[4096,64]{1,0:T(8,128)} fusion(bf16[4096,2,64]{2,1,0:T(2,128)(2,1)} %bitcast.112, pred[4096,2]{1,0:T(8,128)(4,1)S(1)} %copy.79), kind=kLoop, calls=%fused_computation.36 | loop fusion | flops 1310720 | bytes 2105344 | tf_op jit(solution)/shard_map/reduce_sum | solution.py:77
  1272.6 2.2 copy.89
  1274.8 6.9 fusion.41
  1281.7 1.0 add_convert_fusion.1
  1283.4 11.0 bitcast_convert_fusion.1
  1294.4 9.9 bitcast_convert_fusion.2
  1304.4 2.9 convolution_bitcast_fusion
  1307.3 11.3 bitcast_convert_fusion
  1318.6 6.5 copy.95
  1325.1 28.5 %all-gather.8.cloned.1.call-done = bf16[4096,512]{0,1:T(8,128)(2,1)} async-done(((bf16[4096,64]{0,1:T(8,128)(2,1)}), bf16[4096,512]{0,1:T(8,128)(2,1)}) %all-gather.8.cloned.1.call-update) | async-done | bytes 4194320 | tf_op jit(solution)/shard_map/all_gather | solution.py:83
  1353.6 6.4 copy.96
  1360.0 25.9 %all-reduce.2.cloned.1.call-done = f32[512,32]{0,1:T(8,128)} async-done(((f32[512,32]{0,1:T(8,128)}), f32[512,32]{0,1:T(8,128)}) %all-reduce.2.cloned.1.call-update) | async-done | bytes 65552 | tf_op jit(solution)/shard_map/psum | solution.py:81
  1385.9 1.5 copy.130
  (93 shorter events, 3.3 us)
Async XLA Ops:
  7.2 527.3 %copy-start = (bf16[8,128,512]{2,1,0:T(8,128)(2,1)S(1)}, bf16[8,128,512]{2,1,0:T(8,128)(2,1)}, u32[]{:S(2)}) copy-start(bf16[8,128,512]{2,1,0:T(8,128)(2,1)} %param.16) | copy-start | bytes 3145732
  7.2 35.0 %copy-start.22 = (f32[512,32]{0,1:T(8,128)S(1)}, f32[512,32]{0,1:T(8,128)}, u32[]{:S(2)}) copy-start(f32[512,32]{0,1:T(8,128)} %param.11) | copy-start | bytes 196612
  7.2 527.3 %all-gather.6.cloned.1.call-start = ((), (), s32[]{:S(2)}) async-start(), calls=%async_computation.8 | async-start | bytes 18874368 | tf_op jit(solution)/shard_map/all_gather | solution.py:63
  8.8 0.6 copy-start.16
  10.0 39.6 %copy-start.14 = (s32[4096,2]{0,1:T(2,128)S(1)}, s32[4096,2]{0,1:T(2,128)}, u32[]{:S(2)}) copy-start(s32[4096,2]{0,1:T(2,128)} %param.12) | copy-start | bytes 98308
  48.1 0.8 copy-start.5
  48.1 1.8 copy-start.10
  48.9 0.7 copy-start.12
  49.9 0.6 copy-start.20
  49.9 0.6 copy-start.24
  50.5 0.6 copy-start.18
  145.2 58.1 %copy-start.3 = (bf16[4096,64]{1,0:T(8,128)(2,1)}, bf16[4096,64]{1,0:T(8,128)(2,1)S(1)}, u32[]{:S(2)}) copy-start(bf16[4096,64]{1,0:T(8,128)(2,1)S(1)} %constant_dynamic-slice_fusion) | copy-start | bytes 1572868
  241.1 641.5 %reduce-scatter.3.cloned.1.call-start = ((), (), s32[]{:S(2)}) async-start(), calls=%async_computation.6 | async-start | bytes 18874368 | tf_op jit(solution)/shard_map/reduce_scatter | solution.py:50
  319.9 187.5 %copy-start.8 = (bf16[8,512,128]{2,1,0:T(8,128)(2,1)S(1)}, bf16[8,512,128]{2,1,0:T(8,128)(2,1)}, u32[]{:S(2)}) copy-start(bf16[8,512,128]{2,1,0:T(8,128)(2,1)} %param.15) | copy-start | bytes 3145732
  507.4 13.6 copy-start.9
  603.5 561.0 %reduce-scatter.5.cloned.1.call-start = ((), (), s32[]{:S(2)}) async-start(), calls=%async_computation.9 | async-start | bytes 18874368 | tf_op jit(solution)/shard_map/reduce_scatter | solution.py:74
  666.1 1.2 copy-start.4
  668.6 221.9 %copy-start.17 = (s32[4096,2]{0,1:T(2,128)S(1)}, s32[4096,2]{0,1:T(2,128)}, u32[]{:S(2)}) copy-start(s32[4096,2]{0,1:T(2,128)} %copy-done.16) | copy-start | bytes 98308
  886.7 8.5 copy-start.19
  886.7 29.2 %all-to-all-start.1 = ((bf16[4,8,512,64]{2,3,1,0:T(8,128)(2,1)}), bf16[4,8,512,64]{2,3,1,0:T(8,128)(2,1)S(1)}, u32[]{:S(2)}, u32[]{:S(2)}) async-start(bf16[4,8,512,64]{2,3,1,0:T(8,128)(2,1)} %copy.74), calls=%async_computation.2 | async-start | bytes 4194304 | tf_op jit(solution)/shard_map/all_to_all | solution.py:51
  890.5 428.1 %all-gather.4.cloned.1.call-start = ((), (), s32[]{:S(2)}) async-start(), calls=%async_computation.7 | async-start | bytes 4718592 | tf_op jit(solution)/shard_map/all_gather | solution.py:54
  919.1 28.5 %copy-start.26 = (pred[4096,2]{0,1:T(4,128)(4,1)S(1)}, pred[4096,2]{0,1:T(4,128)(4,1)}, u32[]{:S(2)}) copy-start(pred[4096,2]{0,1:T(4,128)(4,1)} %get-tuple-element.42) | copy-start | bytes 24580
  943.7 6.9 copy-start.15
  943.7 7.2 copy-start.27
  943.7 13.3 copy-start.13
  957.0 217.6 %copy-start.25 = (f32[4096]{0:T(1024)S(1)}, f32[4096]{0:T(1024)}, u32[]{:S(2)}) copy-start(f32[4096]{0:T(1024)} %copy-done.24) | copy-start | bytes 49156
  957.0 254.2 %copy-start.21 = (f32[4096,2]{0,1:T(2,128)S(1)}, f32[4096,2]{0,1:T(2,128)}, u32[]{:S(2)}) copy-start(f32[4096,2]{0,1:T(2,128)} %copy-done.20) | copy-start | bytes 98308
  957.0 254.5 %copy-start.6 = (f32[4096,32]{0,1:T(8,128)S(1)}, f32[4096,32]{0,1:T(8,128)}, u32[]{:S(2)}) copy-start(f32[4096,32]{0,1:T(8,128)} %copy-done.5) | copy-start | bytes 1572868
  957.0 254.5 %copy-start.11 = (f32[4096]{0:T(1024)S(1)}, f32[4096]{0:T(1024)}, u32[]{:S(2)}) copy-start(f32[4096]{0:T(1024)} %copy-done.10) | copy-start | bytes 49156
  1168.6 43.1 %all-to-all-start.3 = ((bf16[4,8,512,64]{2,3,1,0:T(8,128)(2,1)}), bf16[4,8,512,64]{2,3,1,0:T(8,128)(2,1)}, u32[]{:S(2)}, u32[]{:S(2)}) async-start(bf16[4,8,512,64]{2,3,1,0:T(8,128)(2,1)} %copy.85), calls=%async_computation.5 | async-start | bytes 4194304 | tf_op jit(solution)/shard_map/all_to_all | solution.py:75
  1173.1 180.5 %all-gather.8.cloned.1.call-start = ((), (), s32[]{:S(2)}) async-start(), calls=%async_computation.10 | async-start | bytes 4718592 | tf_op jit(solution)/shard_map/all_gather | solution.py:83
  1247.4 27.4 %copy-start.23 = (f32[512,32]{0,1:T(8,128)S(1)}, f32[512,32]{0,1:T(8,128)}, u32[]{:S(2)}) copy-start(f32[512,32]{0,1:T(8,128)} %param.11) | copy-start | bytes 196612
  1282.7 103.2 %all-reduce.2.cloned.1.call-start = ((), (), s32[]{:S(2)}) async-start(), calls=%async_computation.11 | async-start | bytes 131072 | tf_op jit(solution)/shard_map/psum | solution.py:81
  1283.4 11.0 copy-start.7
  1294.4 9.9 copy-start.2
  1318.6 68.8 %copy-start.1 = (bf16[8,128,512]{2,1,0:T(8,128)(2,1)S(1)}, bf16[8,128,512]{2,1,0:T(8,128)(2,1)}, u32[]{:S(2)}) copy-start(bf16[8,128,512]{2,1,0:T(8,128)(2,1)} %param.16) | copy-start | bytes 3145732
Sparse Core Ops, SparseCore 0:
  241.2 226.9 all-gather.5
  603.7 278.8 reduce-scatter.2
  886.4 278.0 reduce-scatter.4
  1166.5 73.1 all-gather.3
  1282.8 70.7 all-gather.7
  1356.3 29.5 all-reduce.1
where the time goes:
time: 1410 us; the launch traced here: 1400 us
  waiting for transfers between devices  497 us (35%)
  local copies, waits for them, and re-layouts  422 us (30%)
  blocking collectives  260 us (18%)
  matrix products  149 us (11%)
  other arithmetic  42.8 us (3%)
  between operations  16.9 us (1%)
    reduce_scatter x1, waiting for transfers between devices, device_step(): out_cols = lax.psum_scatter(out_part, 'tp', scatter_dimension=3, tiled=True)  214 us
    reduce_scatter x1, waiting for transfers between devices, device_step(): lax.psum_scatter(d_recv, 'tp', scatter_dimension=3, tiled=True)  207 us
    all_to_all x1, blocking collectives, device_step(): lax.all_to_all(send_rows.reshape(ep_size, exp_local, capacity, d_model),...  187 us
    gather x1, local copies, waits for them, and re-layouts, device_step(): jnp.take(gate_vals.reshape(-1), choice_ids, axis=0, mode='fill', fill_val...  90.5 us
    gather x1, local copies, waits for them, and re-layouts, device_step(): send_rows = jnp.take(x_loc, token_ids, axis=0, mode='fill', fill_value=0)  69.6 us
    gather x2, local copies, waits for them, and re-layouts, device_step(): dy_at_slot = jnp.take(dy_cols, token_ids, axis=0, mode='fill', fill_value=0)  62.7 us
    psum x1, blocking collectives, device_step(): d_gates = lax.psum(gate_part, 'tp')  36.6 us
    gather x1, local copies, waits for them, and re-layouts, device_step(): d_choice = jnp.take(d_send, flat_pos, axis=0, mode='fill', fill_value=0)  30.9 us
  transfers between devices with their start and end apart: 8, of which 5 were waited for; matrix products, arithmetic and copies ran while one was open for 24% of the time, Pallas kernels for 0%

commit v1 on v0

v1 whole, which is shorter than its diff:
```python
import functools

import jax
import jax.numpy as jnp
from jax import lax
from jax.experimental import pallas as pl
from jax.experimental.pallas import tpu as pltpu
from jax.sharding import PartitionSpec as P

AUX_WEIGHT = 0.01
F32 = jnp.float32
BF16 = jnp.bfloat16
VMEM_LIMIT = 64000 * 1024
GELU_C = 0.7978845608028654
GELU_A = 0.044715
ANY = pl.ANY


def dot_nn(a, b):
    return lax.dot_general(a, b, (((1,), (0,)), ((), ())), preferred_element_type=F32)


def dot_nt(a, b):
    return lax.dot_general(a, b, (((1,), (1,)), ((), ())), preferred_element_type=F32)


def dot_tn(a, b):
    return lax.dot_general(a, b, (((0,), (0,)), ((), ())), preferred_element_type=F32)


def split3(v):
    hi = v.astype(BF16)
    rest = v - hi.astype(F32)
    mid = rest.astype(BF16)
    lo = (rest - mid.astype(F32)).astype(BF16)
    return hi, mid, lo


def remote(src, dst, send_sem, recv_sem, tp, ep):
    return pltpu.make_async_remote_copy(
        src_ref=src, dst_ref=dst, send_sem=send_sem, recv_sem=recv_sem,
        device_id={"tp": tp, "ep": ep}, device_id_type=pl.DeviceIdType.MESH,
    )


def dispatch_kernel(n_tp, n_ep, cap, x_ref, dy_ref, idx_ref, key_ref, wgt_ref, w0_ref, w1_ref, wo_ref,
                    r_out, d_out, w0_out, w1_out, wo_out, prob_out, gate_out, stat_out,
                    rbuf, dbuf, stat_buf, acc_r, acc_d, w_send, w_recv, row_send, row_recv, st_send, st_recv, loc_sem):
    s = lax.axis_index("tp")
    q = lax.axis_index("ep")
    tokens = x_ref.shape[0]
    experts = n_tp * n_ep
    weights = ((w0_ref, w0_out), (w1_ref, w1_out), (wo_ref, wo_out))
    copies = []
    for a, (src, dst) in enumerate(weights):
        for p in range(1, n_tp):
            peer = lax.rem(s + p, n_tp)
            copies.append(remote(src.at[peer], dst.at[s], w_send.at[a, p], w_recv.at[a, p], peer, q))
            copies[-1].start()
    local = []
    for a, (src, dst) in enumerate(weights):
        local.append(pltpu.make_async_copy(src.at[s], dst.at[s], loc_sem.at[a]))
        local[-1].start()

    hi, mid, lo = split3(wgt_ref[...])
    parts = jnp.concatenate([hi, mid, lo], axis=0)
    chunk = 1024
    e_iota = lax.broadcasted_iota(jnp.int32, (experts, chunk), 0)
    psum = jnp.zeros((experts, 1), F32)
    count = jnp.zeros((experts, 1), F32)
    for c in range(tokens // chunk):
        cols = pl.ds(c * chunk, chunk)
        lg = dot_nt(parts, x_ref[cols, :])
        logits = lg[:experts] + (lg[experts:2 * experts] + lg[2 * experts:])
        ex = jnp.exp(logits - jnp.max(logits, axis=0, keepdims=True))
        prob = ex / jnp.sum(ex, axis=0, keepdims=True)
        prob_out[:, cols] = prob
        hot1 = e_iota == idx_ref[0:1, cols]
        hot2 = e_iota == idx_ref[1:2, cols]
        g1 = jnp.sum(jnp.where(hot1, prob, 0.0), axis=0, keepdims=True)
        g2 = jnp.sum(jnp.where(hot2, prob, 0.0), axis=0, keepdims=True)
        total = g1 + g2
        gate_out[0:1, cols] = g1 / total
        gate_out[1:2, cols] = g2 / total
        gate_out[2:3, cols] = total
        psum = psum + jnp.sum(prob, axis=1, keepdims=True)
        count = count + jnp.sum(jnp.where(hot1, 1.0, 0.0), axis=1, keepdims=True)
    lane = lax.broadcasted_iota(jnp.int32, (experts, 128), 1)
    stat_buf[...] = jnp.where(lane == 0, count, jnp.where(lane == 1, psum, 0.0))
    for p in range(1, n_ep):
        copies.append(remote(stat_buf, stat_out.at[q], st_send.at[p], st_recv.at[p], s, lax.rem(q + p, n_ep)))
        copies[-1].start()
    local.append(pltpu.make_async_copy(stat_buf, stat_out.at[q], loc_sem.at[3]))
    local[-1].start()

    def row_copies(p, r):
        return (remote(rbuf.at[p], r_out.at[q], row_send.at[0, p], row_recv.at[0, p], s, r),
                remote(dbuf.at[p], d_out.at[q], row_send.at[1, p], row_recv.at[1, p], s, r))

    def own_copies():
        return (pltpu.make_async_copy(rbuf.at[0], r_out.at[q], loc_sem.at[4]),
                pltpu.make_async_copy(dbuf.at[0], d_out.at[q], loc_sem.at[5]))

    tchunk = 512

    def do_dest(i, _):
        p = lax.rem(i + 1, n_ep)
        r = lax.rem(q + p, n_ep)
        base = (r * n_tp + s) * cap
        acc_r[...] = jnp.zeros_like(acc_r)
        acc_d[...] = jnp.zeros_like(acc_d)

        def do_chunk(c, gsum):
            cols = pl.ds(pl.multiple_of(c * tchunk, tchunk), tchunk)
            slot = lax.broadcasted_iota(jnp.int32, (cap, tchunk), 0)
            m1 = (key_ref[0:1, cols] - base) == slot
            m2 = (key_ref[1:2, cols] - base) == slot
            pick = jnp.where(m1 | m2, 1.0, 0.0).astype(BF16)
            acc_r[...] += dot_nn(pick, x_ref[cols, :])
            acc_d[...] += dot_nn(pick, dy_ref[cols, :])
            gsel = jnp.where(m1, gate_out[0:1, cols], 0.0) + jnp.where(m2, gate_out[1:2, cols], 0.0)
            return gsum + jnp.sum(gsel, axis=1, keepdims=True)

        gsum = lax.fori_loop(0, tokens // tchunk, do_chunk, jnp.zeros((cap, 1), F32))
        rbuf[p] = acc_r[...].astype(BF16)
        dbuf[p] = (acc_d[...] * gsum).astype(BF16)

        @pl.when(p > 0)
        def _():
            for cp in row_copies(p, r):
                cp.start()

        @pl.when(p == 0)
        def _():
            for cp in own_copies():
                cp.start()

        return 0

    lax.fori_loop(0, n_ep, do_dest, 0)
    for cp in own_copies():
        cp.wait()
    for cp in local:
        cp.wait()
    for p in range(1, n_ep):
        for cp in row_copies(p, lax.rem(q + p, n_ep)):
            cp.wait()
    for cp in copies:
        cp.wait()


def expert_kernel(n_tp, r_ref, d_ref, w0_ref, w1_ref, wo_ref, rows_out, g0_out, g1_out, go_out,
                  w0c, w1c, h_s, da_s, db_s, acc0, acc1, acco):
    step = pl.program_id(0)
    rows, d_model = r_ref.shape[1], r_ref.shape[2]
    width = wo_ref.shape[0]
    part = width // n_tp

    @pl.when(step == 0)
    def _():
        for j in range(n_tp):
            w0c[:, j * part:(j + 1) * part] = w0_ref[j]
            w1c[:, j * part:(j + 1) * part] = w1_ref[j]
        acc0[...] = jnp.zeros_like(acc0)
        acc1[...] = jnp.zeros_like(acc1)
        acco[...] = jnp.zeros_like(acco)

    r = r_ref[0]
    d = d_ref[0]
    blk = 256
    for j in range(width // blk):
        sl = slice(j * blk, (j + 1) * blk)
        a = dot_nn(r, w0c[:, sl])
        b = dot_nn(r, w1c[:, sl])
        dh = dot_nt(d, wo_ref[sl, :])
        a2 = a * a
        t = jnp.tanh(GELU_C * (a + GELU_A * (a2 * a)))
        cdf = 0.5 * (1.0 + t)
        g = a * cdf
        h_s[:, sl] = (g * b).astype(BF16)
        db_s[:, sl] = (dh * g).astype(BF16)
        slope = cdf + a * (0.5 * (1.0 - t * t) * (GELU_C * (1.0 + (3.0 * GELU_A) * a2)))
        da_s[:, sl] = (dh * b * slope).astype(BF16)
    o = dot_nn(h_s[...], wo_ref[...]).astype(BF16).astype(F32)
    dr = (dot_nt(da_s[...], w0c[...]) + dot_nt(db_s[...], w1c[...])).astype(BF16).astype(F32)
    low = lax.broadcasted_iota(jnp.int32, (rows, 128), 1) < 64
    for j in range(d_model // 128):
        o_blk = o[:, j * 128:(j + 1) * 128]
        r_blk = dr[:, j * 128:(j + 1) * 128]
        rows_out[2 * j, 0] = jnp.where(low, o_blk, pltpu.roll(r_blk, 64, 1)).astype(BF16)
        rows_out[2 * j + 1, 0] = jnp.where(low, pltpu.roll(o_blk, 64, 1), r_blk).astype(BF16)
    acco[...] += dot_tn(h_s[...], d)
    acc0[...] += dot_tn(r, da_s[...])
    acc1[...] += dot_tn(r, db_s[...])

    @pl.when(step == pl.num_programs(0) - 1)
    def _():
        for j in range(n_tp):
            g0_out[j] = acc0[:, j * part:(j + 1) * part].astype(BF16)
            g1_out[j] = acc1[:, j * part:(j + 1) * part].astype(BF16)
        go_out[...] = acco[...].astype(BF16)


def exchange_kernel(n_tp, n_ep, rows_ref, table_out, send, recv, loc):
    s = lax.axis_index("tp")
    q = lax.axis_index("ep")
    me = s * n_ep + q
    copies = []
    for a in range(n_tp):
        for b in range(n_ep):
            if a == 0 and b == 0:
                continue
            tp, ep = lax.rem(s + a, n_tp), lax.rem(q + b, n_ep)
            copies.append(remote(rows_ref.at[tp, ep], table_out.at[me], send.at[a, b], recv.at[a, b], tp, ep))
            copies[-1].start()
    own = pltpu.make_async_copy(rows_ref.at[s, q], table_out.at[me], loc)
    own.start()
    own.wait()
    for cp in copies:
        cp.wait()


def combine_kernel(pos_ref, table_ref, gate_ref, dy_ref, y_out, dr_out, dg_out, tab, c1, c2):
    s = lax.axis_index("tp")
    slots = table_ref.shape[0]
    tokens = dy_ref.shape[0]
    half = tokens // 2
    step = 2048

    def widen(i, _):
        sl = pl.ds(pl.multiple_of(i * step, step), step)
        tab[sl, :] = table_ref[sl, :].astype(F32)
        return 0

    lax.fori_loop(0, slots // step, widen, 0)
    tab[pl.ds(slots, 8), :] = jnp.zeros((8, 128), F32)

    unroll = 16

    def look(i, _):
        t0 = i * unroll
        for u in range(unroll):
            c1[pl.ds(t0 + u, 1), :] = tab[pl.ds(pos_ref[t0 + u], 1), :]
            c2[pl.ds(t0 + u, 1), :] = tab[pl.ds(pos_ref[tokens + t0 + u], 1), :]
        return 0

    lax.fori_loop(0, tokens // unroll, look, 0)

    blk = 512
    low = lax.broadcasted_iota(jnp.int32, (blk, 128), 1) < 64
    odd = lax.rem(s, 2) == 1
    for i in range(half // blk):
        pieces = []
        for h in range(2):
            t0 = h * half + i * blk
            a1 = c1[t0:t0 + blk, :]
            a2 = c2[t0:t0 + blk, :]
            dy = dy_ref[t0:t0 + blk, :].astype(F32)
            dy = jnp.where(odd, pltpu.roll(dy, 64, 1), dy)
            y = gate_ref[t0:t0 + blk, 0:1] * a1 + gate_ref[t0:t0 + blk, 1:2] * a2
            pieces.append((y, a1 + a2))
            for k, av in enumerate((a1, a2)):
                prod = jnp.where(low, dy * av, 0.0)
                line = jnp.sum(prod.T, axis=0, keepdims=True)
                row = k * 4 + t0 // 1024
                col = t0 % 1024
                dg_out[row:row + 1, col:col + blk] = line
        (ya, da), (yb, db) = pieces
        y_out[i * blk:(i + 1) * blk, :] = jnp.where(low, ya, pltpu.roll(yb, 64, 1)).astype(BF16)
        dr_out[i * blk:(i + 1) * blk, :] = jnp.where(low, pltpu.roll(da, 64, 1), db)


def return_kernel(n_tp, n_ep, y_ref, dr_ref, dg_ref, prob_ref, gate_ref, idx_ref, stat_ref, x_ref, wgt_ref,
                  g0_ref, g1_ref, go_ref,
                  gy_out, gx_out, g0_out, g1_out, go_out, dwg_out, aux_out,
                  dg_all, dx_buf, dl_buf, dwg_buf, dwg_all,
                  g_send, g_recv, dg_send, dg_recv, ag_send, ag_recv, wg_send, wg_recv, loc):
    s = lax.axis_index("tp")
    q = lax.axis_index("ep")
    n_z = n_tp // 2
    z = s // 2
    y = lax.rem(s, 2)
    tokens = x_ref.shape[0]
    experts = n_tp * n_ep
    total_tokens = float(tokens * n_ep)
    half = tokens // 2
    copies = []
    for p in range(1, n_tp):
        peer = lax.rem(s + p, n_tp)
        copies.append(remote(dg_ref, dg_all.at[s], dg_send.at[p], dg_recv.at[p], peer, q))
        copies[-1].start()
    dg_copies = list(copies)
    dg_own = pltpu.make_async_copy(dg_ref, dg_all.at[s], loc.at[0])
    dg_own.start()

    class Gather:
        def __init__(self, a, out):
            self.a, self.out = a, out

        def hop(self, src, owner, way, tp):
            return remote(src, self.out.at[owner], ag_send.at[self.a, owner, way], ag_recv.at[self.a, owner], tp, q)

        def up(self, src, owner):
            return self.hop(src, owner, 0, lax.rem(s + 2, n_tp))

        def down(self, src, owner):
            return self.hop(src, owner, 1, lax.rem(s + n_tp - 2, n_tp))

        def across(self, src, owner):
            return self.hop(src, owner, 2, s + 1 - 2 * y)

        def begin(self, src):
            self.src = src
            self.own = pltpu.make_async_copy(src, self.out.at[s], loc.at[1 + self.a])

            @pl.when(z < n_z - 1)
            def _():
                self.up(src, s).start()

            @pl.when(z > 0)
            def _():
                self.down(src, s).start()

            self.across(src, s).start()
            self.own.start()

        def relay(self, dist):
            @pl.when(z >= dist)
            def _():
                owner = lax.rem(s + n_tp - 2 * dist, n_tp)
                blk = self.out.at[owner]
                self.up(blk, owner).wait_recv()

                @pl.when(z < n_z - 1)
                def _():
                    self.up(blk, owner).start()

                self.across(blk, owner).start()

            @pl.when(z + dist < n_z)
            def _():
                owner = lax.rem(s + 2 * dist, n_tp)
                blk = self.out.at[owner]
                self.down(blk, owner).wait_recv()

                @pl.when(z > 0)
                def _():
                    self.down(blk, owner).start()

                self.across(blk, owner).start()

        def finish(self):
            @pl.when(z < n_z - 1)
            def _():
                self.up(self.src, s).wait_send()

            @pl.when(z > 0)
            def _():
                self.down(self.src, s).wait_send()

            self.across(self.src, s).wait_send()
            self.own.wait()
            for dist in range(1, n_z):
                @pl.when(z >= dist)
                def _():
                    owner = lax.rem(s + n_tp - 2 * dist, n_tp)
                    blk = self.out.at[owner]

                    @pl.when(z < n_z - 1)
                    def _():
                        self.up(blk, owner).wait_send()

                    self.across(blk, owner).wait_send()

                @pl.when(z + dist < n_z)
                def _():
                    owner = lax.rem(s + 2 * dist, n_tp)
                    blk = self.out.at[owner]

                    @pl.when(z > 0)
                    def _():
                        self.down(blk, owner).wait_send()

                    self.across(blk, owner).wait_send()

            for k in range(n_z):
                owner = 2 * k + 1 - y
                self.across(self.out.at[owner], owner).wait_recv()

    gat_y = Gather(0, gy_out)
    gat_x = Gather(1, gx_out)
    gat_y.begin(y_ref)

    grads = ((g0_ref, g0_out), (g1_ref, g1_out), (go_ref, go_out))
    local = [dg_own]
    for a, (src, dst) in enumerate(grads):
        for p in range(1, n_tp):
            peer = lax.rem(s + p, n_tp)
            cp = remote(src.at[peer], dst.at[s], g_send.at[a, p], g_recv.at[a, p], peer, q)
            cp.start()
            copies.append(cp)
        local.append(pltpu.make_async_copy(src.at[s], dst.at[s], loc.at[3 + a]))
        local[-1].start()

    counts = stat_ref[0, :, 0:1]
    sums = stat_ref[0, :, 1:2]
    for e in range(1, n_ep):
        counts = counts + stat_ref[e, :, 0:1]
        sums = sums + stat_ref[e, :, 1:2]
    aux_out[...] = jnp.broadcast_to(jnp.sum(counts * sums, axis=0, keepdims=True) * (experts / (total_tokens * total_tokens)), aux_out.shape)
    aux_cot = counts * (AUX_WEIGHT * experts / (total_tokens * total_tokens))
    for cp in dg_copies:
        cp.wait_recv()
    dg_own.wait()
    chunk = 1024
    e_iota = lax.broadcasted_iota(jnp.int32, (experts, chunk), 0)
    for c in range(tokens // chunk):
        cols = pl.ds(c * chunk, chunk)
        dw1 = dg_all[0, c:c + 1, :]
        dw2 = dg_all[0, 4 + c:5 + c, :]
        for o in range(1, n_tp):
            dw1 = dw1 + dg_all[o, c:c + 1, :]
            dw2 = dw2 + dg_all[o, 4 + c:5 + c, :]
        w1 = gate_ref[0:1, cols]
        w2 = gate_ref[1:2, cols]
        tot = gate_ref[2:3, cols]
        mean = dw1 * w1 + dw2 * w2
        dg1 = (dw1 - mean) / tot
        dg2 = (dw2 - mean) / tot
        prob = prob_ref[:, cols]
        dp = jnp.where(e_iota == idx_ref[0:1, cols], dg1, 0.0) + jnp.where(e_iota == idx_ref[1:2, cols], dg2, 0.0) + aux_cot
        dl = prob * (dp - jnp.sum(prob * dp, axis=0, keepdims=True))
        hi, mid, lo = split3(dl)
        dl_buf[0:experts, cols] = hi
        dl_buf[experts:2 * experts, cols] = mid
        dl_buf[2 * experts:, cols] = lo

    whi, wmid, wlo = split3(wgt_ref[...])
    left = lax.broadcasted_iota(jnp.int32, (half, 128), 1) < 64
    w_top = jnp.concatenate([whi, whi, whi], axis=0)
    w_mid = jnp.concatenate([wmid, wmid], axis=0)
    dl_all = dl_buf[...]
    xr = dot_tn(dl_all, w_top) + dot_tn(dl_all[:2 * experts], w_mid) + dot_tn(dl_all[:experts], wlo)
    xr = jnp.where(left, xr[:half], pltpu.roll(xr[half:], 64, 1))
    dx_buf[...] = (dr_ref[...] + xr).astype(BF16)
    gat_x.begin(dx_buf)
    gat_y.relay(1)
    dw = dot_nn(dl_all, x_ref[...])
    dwg_buf[...] = dw[:experts] + (dw[experts:2 * experts] + dw[2 * experts:])
    wg_copies = []
    for p in range(1, n_ep):
        cp = remote(dwg_buf, dwg_all.at[q], wg_send.at[p], wg_recv.at[p], s, lax.rem(q + p, n_ep))
        cp.start()
        wg_copies.append(cp)
    wg_own = pltpu.make_async_copy(dwg_buf, dwg_all.at[q], loc.at[6])
    wg_own.start()
    gat_y.relay(2)
    gat_x.relay(1)
    gat_y.relay(3)
    gat_x.relay(2)
    gat_x.relay(3)
    wg_own.wait()
    for cp in wg_copies:
        cp.wait()
    tot = dwg_all[0]
    for e in range(1, n_ep):
        tot = tot + dwg_all[e]
    dwg_out[...] = tot
    gat_y.finish()
    gat_x.finish()
    for cp in dg_copies:
        cp.wait_send()
    for cp in local[1:]:
        cp.wait()
    for cp in copies[len(dg_copies):]:
        cp.wait()


def interleave_kernel(gy_ref, gx_ref, y_out, dx_out):
    half = gy_ref.shape[1]
    low = lax.broadcasted_iota(jnp.int32, (half, 128), 1) < 64
    for src, dst in ((gy_ref, y_out), (gx_ref, dx_out)):
        a = src[0].astype(F32)
        b = src[1].astype(F32)
        dst[0:half, :] = jnp.where(low, a, pltpu.roll(b, 64, 1)).astype(BF16)
        dst[half:2 * half, :] = jnp.where(low, pltpu.roll(a, 64, 1), b).astype(BF16)


def solution(mesh):
    n_ep = mesh.shape["ep"]
    n_tp = mesh.shape["tp"]
    vmem = pl.BlockSpec(memory_space=pltpu.VMEM)
    hbm = pl.BlockSpec(memory_space=ANY)
    dma = pltpu.SemaphoreType.DMA
    sds = jax.ShapeDtypeStruct

    def device_step(x_loc, w_router, idx_loc, slot_loc, gelu_loc, lin_loc, out_loc, dy_loc):
        tokens, d_model = x_loc.shape
        exp_local = gelu_loc.shape[0]
        part = gelu_loc.shape[2]
        width = part * n_tp
        experts = exp_local * n_ep
        cap = 4 * tokens // experts
        slots = experts * cap
        s = lax.axis_index("tp")
        idx_t = idx_loc.T
        slot_t = slot_loc.T
        kept = slot_t < cap
        key_t = jnp.where(kept, idx_t * cap + slot_t, -1)
        pos = jnp.where(kept, ((idx_t % n_tp) * n_ep + idx_t // n_tp) * cap + slot_t, slots).reshape(-1)
        wgt = w_router.T
        side = pltpu.CompilerParams(has_side_effects=True, vmem_limit_bytes=VMEM_LIMIT)

        rows, drows, w0, w1, wo, prob, gate, stat = pl.pallas_call(
            functools.partial(dispatch_kernel, n_tp, n_ep, cap),
            name="moe_dispatch",
            out_shape=(sds((n_ep, cap, d_model), BF16), sds((n_ep, cap, d_model), BF16),
                       sds(gelu_loc.shape, BF16), sds(lin_loc.shape, BF16), sds(out_loc.shape, BF16),
                       sds((experts, tokens), F32), sds((8, tokens), F32), sds((n_ep, experts, 128), F32)),
            in_specs=[vmem] * 5 + [hbm] * 3,
            out_specs=(hbm, hbm, hbm, hbm, hbm, vmem, vmem, vmem),
            scratch_shapes=[pltpu.VMEM((n_ep, cap, d_model), BF16), pltpu.VMEM((n_ep, cap, d_model), BF16),
                            pltpu.VMEM((experts, 128), F32), pltpu.VMEM((cap, d_model), F32), pltpu.VMEM((cap, d_model), F32),
                            dma((3, n_tp)), dma((3, n_tp)), dma((2, n_ep)), dma((2, n_ep)), dma((n_ep,)), dma((n_ep,)), dma((6,))],
            compiler_params=side,
        )(x_loc, dy_loc, idx_t, key_t, wgt, gelu_loc, lin_loc, out_loc)

        full = lambda shape: pl.BlockSpec(shape, lambda i: (0,) * len(shape))
        back, g0, g1, go = pl.pallas_call(
            functools.partial(expert_kernel, n_tp),
            name="moe_expert",
            grid=(n_ep,),
            out_shape=(sds((n_tp, n_ep, cap, 128), BF16), sds((n_tp, d_model, part), BF16), sds((n_tp, d_model, part), BF16), sds((width, d_model), BF16)),
            in_specs=[pl.BlockSpec((1, cap, d_model), lambda i: (i, 0, 0)), pl.BlockSpec((1, cap, d_model), lambda i: (i, 0, 0)),
                      full((n_tp, d_model, part)), full((n_tp, d_model, part)), full((width, d_model))],
            out_specs=(pl.BlockSpec((n_tp, 1, cap, 128), lambda i: (0, i, 0, 0)), full((n_tp, d_model, part)), full((n_tp, d_model, part)), full((width, d_model))),
            scratch_shapes=[pltpu.VMEM((d_model, width), BF16), pltpu.VMEM((d_model, width), BF16),
                            pltpu.VMEM((cap, width), BF16), pltpu.VMEM((cap, width), BF16), pltpu.VMEM((cap, width), BF16),
                            pltpu.VMEM((d_model, width), F32), pltpu.VMEM((d_model, width), F32), pltpu.VMEM((width, d_model), F32)],
            compiler_params=pltpu.CompilerParams(dimension_semantics=("arbitrary",), vmem_limit_bytes=VMEM_LIMIT),
        )(rows, drows, w0, w1, wo.reshape(width, d_model))

        table = pl.pallas_call(
            functools.partial(exchange_kernel, n_tp, n_ep),
            name="moe_exchange",
            out_shape=sds((n_tp * n_ep, cap, 128), BF16),
            in_specs=[hbm],
            out_specs=hbm,
            scratch_shapes=[dma((n_tp, n_ep)), dma((n_tp, n_ep)), dma(())],
            compiler_params=side,
        )(back)

        dy_cols = lax.dynamic_slice_in_dim(dy_loc, (s // 2) * 128, 128, axis=1)
        y_pk, dr_pk, dg = pl.pallas_call(
            combine_kernel,
            name="moe_combine",
            out_shape=(sds((tokens // 2, 128), BF16), sds((tokens // 2, 128), F32), sds((8, tokens // 4), F32)),
            in_specs=[pl.BlockSpec(memory_space=pltpu.SMEM), vmem, vmem, vmem],
            out_specs=(vmem, vmem, vmem),
            scratch_shapes=[pltpu.VMEM((slots + 8, 128), F32), pltpu.VMEM((tokens, 128), F32), pltpu.VMEM((tokens, 128), F32)],
            compiler_params=pltpu.CompilerParams(vmem_limit_bytes=VMEM_LIMIT),
        )(pos, table.reshape(slots, 128), gate[:2].T, dy_cols)

        col0 = s * (d_model // n_tp)
        wg_cols = jnp.pad(lax.dynamic_slice_in_dim(wgt, col0, d_model // n_tp, axis=1), ((0, 0), (0, 64)))
        gy, gx, grad_gelu, grad_lin, grad_out, dwg_t, aux = pl.pallas_call(
            functools.partial(return_kernel, n_tp, n_ep),
            name="moe_return",
            out_shape=(sds((n_tp, tokens // 2, 128), BF16), sds((n_tp, tokens // 2, 128), BF16),
                       sds(gelu_loc.shape, BF16), sds(lin_loc.shape, BF16), sds(out_loc.shape, BF16),
                       sds((experts, d_model), F32), sds((8, 128), F32)),
            in_specs=[vmem] * 9 + [hbm] * 3,
            out_specs=(hbm, hbm, hbm, hbm, hbm, vmem, vmem),
            scratch_shapes=[pltpu.VMEM((n_tp, 8, tokens // 4), F32), pltpu.VMEM((tokens // 2, 128), BF16),
                            pltpu.VMEM((3 * experts, tokens), BF16), pltpu.VMEM((experts, d_model), F32), pltpu.VMEM((n_ep, experts, d_model), F32),
                            dma((3, n_tp)), dma((3, n_tp)), dma((n_tp,)), dma((n_tp,)),
                            dma((2, n_tp, 3)), dma((2, n_tp)), dma((n_ep,)), dma((n_ep,)), dma((7,))],
            compiler_params=side,
        )(y_pk, dr_pk, dg, prob, gate, idx_t, stat, x_loc, wg_cols, g0, g1, go.reshape(out_loc.shape))

        pair = pl.BlockSpec((2, tokens // 2, 128), lambda j: (j, 0, 0))
        cols = pl.BlockSpec((tokens, 128), lambda j: (0, j))
        y_loc, dx_loc = pl.pallas_call(
            interleave_kernel,
            name="moe_interleave",
            grid=(n_tp // 2,),
            out_shape=(sds((tokens, d_model), BF16), sds((tokens, d_model), BF16)),
            in_specs=[pair, pair],
            out_specs=(cols, cols),
            compiler_params=pltpu.CompilerParams(dimension_semantics=("arbitrary",), vmem_limit_bytes=VMEM_LIMIT),
        )(gy, gx)
        return y_loc, dx_loc, grad_gelu, grad_lin, grad_out, dwg_t.T, aux[0, 0]

    rows_spec = P("ep", None)
    weight_in = P("ep", None, "tp")
    weight_out = P("ep", "tp", None)
    return jax.shard_map(
        device_step,
        mesh=mesh,
        in_specs=(rows_spec, P(None, None), rows_spec, rows_spec, weight_in, weight_in, weight_out, rows_spec),
        out_specs=(rows_spec, rows_spec, weight_in, weight_in, weight_out, P(None, None), P()),
        check_vma=False,
    )
```

time: 1410 us -> 419 us (0.30)
  waiting for transfers between devices: 497 us -> 0 us
  local copies, waits for them, and re-layouts: 422 us -> 13.3 us
  Pallas kernels: 0 us -> 403 us
  blocking collectives: 260 us -> 0 us
  matrix products: 149 us -> 0 us
  other arithmetic: 42.8 us -> 1.53 us
  between operations: 16.9 us -> 0.69 us
    reduce_scatter x2 -> x0, waiting for transfers between devices: 421 us -> none  [the longest x1 214 us: device_step(): out_cols = lax.psum_scatter(out_part, 'tp', scatter_dimension=3, tiled=True)]
    pallas_call x0 -> x6, Pallas kernels: none -> 403 us  [the longest x1 191 us: device_step(): pl.pallas_call(functools.partial(return_kernel, n_tp, n_ep), name='moe_re...]
    gather x7 -> x0, local copies, waits for them, and re-layouts: 282 us -> none  [the longest x1 90.5 us: device_step(): jnp.take(gate_vals.reshape(-1), choice_ids, axis=0, mode='fill', fill_val...]
    all_to_all x2 -> x0, blocking collectives: 217 us -> none  [the longest x1 187 us: device_step(): lax.all_to_all(send_rows.reshape(ep_size, exp_local, capacity, d_model),...]
    dot_general x12 -> x0, matrix products: 149 us -> none  [the longest x1 20.5 us: device_step(): jnp.einsum('secf,efd->secd', hidden, out_loc, preferred_element_type=jnp....]
    convert_element_type x3 -> x0, local copies, waits for them, and re-layouts: 58.4 us -> none  [the longest x1 28.6 us: device_step(): (d_recv + jnp.einsum('secf,edf->secd', d_pre_lin, lin_loc, preferred_elem...]
    psum x2 -> x0, blocking collectives: 42.7 us -> none  [the longest x1 36.6 us: device_step(): d_gates = lax.psum(gate_part, 'tp')]
    scatter x1 -> x0, local copies, waits for them, and re-layouts: 30.5 us -> none  [device_step(): jnp.full((slots_total,), 2 * shard_tokens, jnp.int32)]
  transfers between devices with their start and end apart: 8 -> 0, of which waited for: 5 -> 0; matrix products, arithmetic and copies ran while one was open for 24% -> 0% of each run, Pallas kernels for 0% -> 0%
where the time goes in v1:
time: 419 us
  Pallas kernels  403 us (96%)
  local copies, waits for them, and re-layouts  13.3 us (3%)
    pallas_call x1, Pallas kernels, device_step(): pl.pallas_call(functools.partial(return_kernel, n_tp, n_ep), name='moe_re...  191 us
    pallas_call x1, Pallas kernels, device_step(): pl.pallas_call(functools.partial(exchange_kernel, n_tp, n_ep), name='moe_...  86.1 us
    pallas_call x1, Pallas kernels, device_step(): pl.pallas_call(functools.partial(dispatch_kernel, n_tp, n_ep, cap), name=...  76.3 us
    pallas_call x1, Pallas kernels, device_step(): pl.pallas_call(functools.partial(expert_kernel, n_tp), name='moe_expert',...  27.3 us
    pallas_call x1, Pallas kernels, device_step(): pl.pallas_call(combine_kernel, name='moe_combine', out_shape=(sds((tokens...  15.5 us

profile of v1, /device:TPU:0, one launch (start us, length us, event | category | flops | bytes accessed | tf_op | source)
XLA Modules:
  0.0 418.8 jit_solution(6846855872368294395)
XLA Ops:
  0.6 0.8 dynamic-slice_bitcast_fusion
  1.4 0.6 pad.4.wgt_ref
  2.1 1.5 fusion.4
  3.6 0.6 copy.16
  4.2 2.3 constant_dynamic-slice_fusion.dy_ref
  6.5 76.3 %moe_dispatch.1 = (bf16[4,512,512]{2,1,0:T(8,128)(2,1)}, bf16[4,512,512]{2,1,0:T(8,128)(2,1)}, bf16[8,512,128]{2,1,0:T(8,128)(2,1)}, bf16[8,512,128]{2,1,0:T(8,1...) custom-call(bf16[4096,512]{1,0:T(8,128)(2,1)} %x_ref.3, ...), custom_call_target="tpu_custom_call" | custom-call | tf_op jit(solution)/shard_map/moe_dispatch/pallas_call | solution.py:514
  82.7 27.3 %moe_expert.1 = (bf16[8,4,512,128]{3,2,1,0:T(8,128)(2,1)}, bf16[8,512,128]{2,1,0:T(8,128)(2,1)}, bf16[8,512,128]{2,1,0:T(8,128)(2,1)}, bf16[1024,512]{1,0:T(8,128)(2,1)}) custom-call(bf16[4,512,512]{2,1,0:T(8,128)(2,1)} %get-tuple-element.31.r_ref, bf16[4,512,512]{2,1,0:T(8,128)(2,1)} %get-tuple-element.32.d_ref, ...), custom_call_target="tpu_custom_call" | custom-call | tf_op jit(solution)/shard_map/moe_expert/pallas_call | solution.py:529
  110.0 86.1 %moe_exchange.1 = bf16[32,512,128]{2,1,0:T(8,128)(2,1)} custom-call(bf16[8,4,512,128]{3,2,1,0:T(8,128)(2,1)} %get-tuple-element.36.rows_ref), custom_call_target="tpu_custom_call" | custom-call | tf_op jit(solution)/shard_map/moe_exchange/pallas_call | solution.py:543
  196.0 0.9 slice.6
  197.0 2.0 copy.15
  198.9 15.5 %moe_combine.1 = (bf16[2048,128]{1,0:T(8,128)(2,1)}, f32[2048,128]{1,0:T(8,128)}, f32[8,1024]{1,0:T(8,128)}) custom-call(s32[8192]{0:T(1024)} %bitcast.35, bf16[16384,128]{1,0:T(8,128)(2,1)} %bitcast.29, f32[4096,2]{1,0:T(8,128)} %bitcast.30, bf16[4096,128]{1,0:T(8,128)(2,1)} %constant_dynamic-slice_fusion.dy_ref), custom_call_target="tpu_custom_call" | custom-call | tf_op jit(solution)/shard_map/moe_combine/pallas_call | solution.py:554
  214.4 190.6 %moe_return.1 = (bf16[8,2048,128]{2,1,0:T(8,128)(2,1)}, bf16[8,2048,128]{2,1,0:T(8,128)(2,1)}, bf16[8,512,128]{2,1,0:T(8,128)(2,1)}, bf16[8,512,128]{2,1,0:T(8,1...) custom-call(bf16[2048,128]{1,0:T(8,128)(2,1)} %get-tuple-element.38.y_ref, ...), custom_call_target="tpu_custom_call" | custom-call | tf_op jit(solution)/shard_map/moe_return/pallas_call | solution.py:566
  405.0 1.2 slice.7
  406.2 0.0 copy-start.1
  406.2 7.6 %moe_interleave.1 = (bf16[4096,512]{1,0:T(8,128)(2,1)}, bf16[4096,512]{1,0:T(8,128)(2,1)}) custom-call(bf16[8,2048,128]{2,1,0:T(8,128)(2,1)} %get-tuple-element.46.gy_ref, bf16[8,2048,128]{2,1,0:T(8,128)(2,1)} %get-tuple-element.47.gx_ref), custom_call_target="tpu_custom_call" | custom-call | tf_op jit(solution)/shard_map/moe_interleave/pallas_call | solution.py:583
  413.9 0.0 copy-start
  413.9 0.0 copy-start.2
  413.9 2.4 copy.21
  416.2 0.0 copy-done.1
  416.2 1.0 copy.22
  417.2 0.0 copy-done
  417.2 1.0 copy.23
  418.2 0.0 copy-done.2
  418.2 0.6 copy.24
Async XLA Ops:
  406.2 10.0 %copy-start.1 = (bf16[8,512,128]{2,1,0:T(8,128)(2,1)S(1)}, bf16[8,512,128]{2,1,0:T(8,128)(2,1)}, u32[]{:S(2)}) copy-start(bf16[8,512,128]{2,1,0:T(8,128)(2,1)} %get-tuple-element.67) | copy-start | bytes 3145732
  413.9 3.3 copy-start
  413.9 4.3 %copy-start.2 = (f32[32,512]{1,0:T(8,128)S(1)}, f32[32,512]{1,0:T(8,128)}, u32[]{:S(2)}) copy-start(f32[32,512]{1,0:T(8,128)} %get-tuple-element.53) | copy-start | bytes 196612

commit v2 on v1

--- a/solution.py
+++ b/solution.py
@@ -44,8 +44,8 @@
 
 
 def dispatch_kernel(n_tp, n_ep, cap, x_ref, dy_ref, idx_ref, key_ref, wgt_ref, w0_ref, w1_ref, wo_ref,
-                    r_out, d_out, w0_out, w1_out, wo_out, prob_out, gate_out, stat_out,
-                    rbuf, dbuf, stat_buf, acc_r, acc_d, w_send, w_recv, row_send, row_recv, st_send, st_recv, loc_sem):
+                    r_out, d_out, w0_out, w1_out, wo_out, prob_out, gate_out, stat_out, dyc_out, gcol_out,
+                    x_buf, dy_buf, rbuf, dbuf, stat_buf, acc_r, acc_d, w_send, w_recv, row_send, row_recv, st_send, st_recv, loc_sem):
     s = lax.axis_index("tp")
     q = lax.axis_index("ep")
     tokens = x_ref.shape[0]
@@ -57,6 +57,10 @@
             peer = lax.rem(s + p, n_tp)
             copies.append(remote(src.at[peer], dst.at[s], w_send.at[a, p], w_recv.at[a, p], peer, q))
             copies[-1].start()
+    x_load = pltpu.make_async_copy(x_ref, x_buf, loc_sem.at[6])
+    dy_load = pltpu.make_async_copy(dy_ref, dy_buf, loc_sem.at[7])
+    x_load.start()
+    dy_load.start()
     local = []
     for a, (src, dst) in enumerate(weights):
         local.append(pltpu.make_async_copy(src.at[s], dst.at[s], loc_sem.at[a]))
@@ -68,9 +72,10 @@
     e_iota = lax.broadcasted_iota(jnp.int32, (experts, chunk), 0)
     psum = jnp.zeros((experts, 1), F32)
     count = jnp.zeros((experts, 1), F32)
+    x_load.wait()
     for c in range(tokens // chunk):
         cols = pl.ds(c * chunk, chunk)
-        lg = dot_nt(parts, x_ref[cols, :])
+        lg = dot_nt(parts, x_buf[cols, :])
         logits = lg[:experts] + (lg[experts:2 * experts] + lg[2 * experts:])
         ex = jnp.exp(logits - jnp.max(logits, axis=0, keepdims=True))
         prob = ex / jnp.sum(ex, axis=0, keepdims=True)
@@ -83,6 +88,7 @@
         gate_out[0:1, cols] = g1 / total
         gate_out[1:2, cols] = g2 / total
         gate_out[2:3, cols] = total
+        gate_out[3:8, cols] = jnp.zeros((5, chunk), F32)
         psum = psum + jnp.sum(prob, axis=1, keepdims=True)
         count = count + jnp.sum(jnp.where(hot1, 1.0, 0.0), axis=1, keepdims=True)
     lane = lax.broadcasted_iota(jnp.int32, (experts, 128), 1)
@@ -102,6 +108,7 @@
                 pltpu.make_async_copy(dbuf.at[0], d_out.at[q], loc_sem.at[5]))
 
     tchunk = 512
+    dy_load.wait()
 
     def do_dest(i, _):
         p = lax.rem(i + 1, n_ep)
@@ -116,8 +123,8 @@
             m1 = (key_ref[0:1, cols] - base) == slot
             m2 = (key_ref[1:2, cols] - base) == slot
             pick = jnp.where(m1 | m2, 1.0, 0.0).astype(BF16)
-            acc_r[...] += dot_nn(pick, x_ref[cols, :])
-            acc_d[...] += dot_nn(pick, dy_ref[cols, :])
+            acc_r[...] += dot_nn(pick, x_buf[cols, :])
+            acc_d[...] += dot_nn(pick, dy_buf[cols, :])
             gsel = jnp.where(m1, gate_out[0:1, cols], 0.0) + jnp.where(m2, gate_out[1:2, cols], 0.0)
             return gsum + jnp.sum(gsel, axis=1, keepdims=True)
 
@@ -138,6 +145,14 @@
         return 0
 
     lax.fori_loop(0, n_ep, do_dest, 0)
+
+    pair = pl.ds(pl.multiple_of((s // 2) * 128, 128), 128)
+    odd = lax.rem(s, 2) == 1
+    for c in range(tokens // chunk):
+        cols = pl.ds(c * chunk, chunk)
+        dyc = dy_buf[cols, pair].astype(F32)
+        dyc_out[cols, :] = jnp.where(odd, pltpu.roll(dyc, 64, 1), dyc).astype(BF16)
+        gcol_out[cols, :] = gate_out[:, cols].T
     for cp in own_copies():
         cp.wait()
     for cp in local:
@@ -149,130 +164,86 @@
         cp.wait()
 
 
-def expert_kernel(n_tp, r_ref, d_ref, w0_ref, w1_ref, wo_ref, rows_out, g0_out, g1_out, go_out,
-                  w0c, w1c, h_s, da_s, db_s, acc0, acc1, acco):
-    step = pl.program_id(0)
+def expert_kernel(n_tp, n_ep, r_ref, d_ref, w0_ref, w1_ref, wo_ref, table_out, g0_out, g1_out, go_out,
+                  w0c, w1c, h_s, da_s, db_s, acc0, acc1, acco, back, send, recv, loc):
+    s = lax.axis_index("tp")
+    q = lax.axis_index("ep")
+    me = s * n_ep + q
     rows, d_model = r_ref.shape[1], r_ref.shape[2]
     width = wo_ref.shape[0]
     part = width // n_tp
-
-    @pl.when(step == 0)
-    def _():
-        for j in range(n_tp):
-            w0c[:, j * part:(j + 1) * part] = w0_ref[j]
-            w1c[:, j * part:(j + 1) * part] = w1_ref[j]
-        acc0[...] = jnp.zeros_like(acc0)
-        acc1[...] = jnp.zeros_like(acc1)
-        acco[...] = jnp.zeros_like(acco)
-
-    r = r_ref[0]
-    d = d_ref[0]
-    blk = 256
-    for j in range(width // blk):
-        sl = slice(j * blk, (j + 1) * blk)
-        a = dot_nn(r, w0c[:, sl])
-        b = dot_nn(r, w1c[:, sl])
-        dh = dot_nt(d, wo_ref[sl, :])
-        a2 = a * a
-        t = jnp.tanh(GELU_C * (a + GELU_A * (a2 * a)))
-        cdf = 0.5 * (1.0 + t)
-        g = a * cdf
-        h_s[:, sl] = (g * b).astype(BF16)
-        db_s[:, sl] = (dh * g).astype(BF16)
-        slope = cdf + a * (0.5 * (1.0 - t * t) * (GELU_C * (1.0 + (3.0 * GELU_A) * a2)))
-        da_s[:, sl] = (dh * b * slope).astype(BF16)
-    o = dot_nn(h_s[...], wo_ref[...]).astype(BF16).astype(F32)
-    dr = (dot_nt(da_s[...], w0c[...]) + dot_nt(db_s[...], w1c[...])).astype(BF16).astype(F32)
-    low = lax.broadcasted_iota(jnp.int32, (rows, 128), 1) < 64
-    for j in range(d_model // 128):
-        o_blk = o[:, j * 128:(j + 1) * 128]
-        r_blk = dr[:, j * 128:(j + 1) * 128]
-        rows_out[2 * j, 0] = jnp.where(low, o_blk, pltpu.roll(r_blk, 64, 1)).astype(BF16)
-        rows_out[2 * j + 1, 0] = jnp.where(low, pltpu.roll(o_blk, 64, 1), r_blk).astype(BF16)
-    acco[...] += dot_tn(h_s[...], d)
-    acc0[...] += dot_tn(r, da_s[...])
-    acc1[...] += dot_tn(r, db_s[...])
-
-    @pl.when(step == pl.num_programs(0) - 1)
-    def _():
-        for j in range(n_tp):
-            g0_out[j] = acc0[:, j * part:(j + 1) * part].astype(BF16)
-            g1_out[j] = acc1[:, j * part:(j + 1) * part].astype(BF16)
-        go_out[...] = acco[...].astype(BF16)
-
-
-def exchange_kernel(n_tp, n_ep, rows_ref, table_out, send, recv, loc):
-    s = lax.axis_index("tp")
-    q = lax.axis_index("ep")
-    me = s * n_ep + q
-    copies = []
-    for a in range(n_tp):
-        for b in range(n_ep):
-            if a == 0 and b == 0:
-                continue
-            tp, ep = lax.rem(s + a, n_tp), lax.rem(q + b, n_ep)
-            copies.append(remote(rows_ref.at[tp, ep], table_out.at[me], send.at[a, b], recv.at[a, b], tp, ep))
-            copies[-1].start()
-    own = pltpu.make_async_copy(rows_ref.at[s, q], table_out.at[me], loc)
-    own.start()
+    for j in range(n_tp):
+        w0c[:, j * part:(j + 1) * part] = w0_ref[j]
+        w1c[:, j * part:(j + 1) * part] = w1_ref[j]
+    acc0[...] = jnp.zeros_like(acc0)
+    acc1[...] = jnp.zeros_like(acc1)
+    acco[...] = jnp.zeros_like(acco)
+
+    def row_copy(a, b):
+        tp, ep = lax.rem(s + a, n_tp), lax.rem(q + b, n_ep)
+        return remote(back.at[tp, ep], table_out.at[me], send.at[a, b], recv.at[a, b], tp, ep)
+
+    own = pltpu.make_async_copy(back.at[s, q], table_out.at[me], loc)
+
+    def shard(i, _):
+        b = lax.rem(i + 1, n_ep)
+        ep = lax.rem(q + b, n_ep)
+        r = r_ref[ep]
+        d = d_ref[ep]
+        blk = 256
+        for j in range(width // blk):
+            sl = slice(j * blk, (j + 1) * blk)
+            u = dot_nn(r, w0c[:, sl])
+            v = dot_nn(r, w1c[:, sl])
+            dh = dot_nt(d, wo_ref[sl, :])
+            u2 = u * u
+            t = jnp.tanh(GELU_C * (u + GELU_A * (u2 * u)))
+            cdf = 0.5 * (1.0 + t)
+            g = u * cdf
+            h_s[:, sl] = (g * v).astype(BF16)
+            db_s[:, sl] = (dh * g).astype(BF16)
+            slope = cdf + u * (0.5 * (1.0 - t * t) * (GELU_C * (1.0 + (3.0 * GELU_A) * u2)))
+            da_s[:, sl] = (dh * v * slope).astype(BF16)
+        o = dot_nn(h_s[...], wo_ref[...]).astype(BF16).astype(F32)
+        dr = (dot_nt(da_s[...], w0c[...]) + dot_nt(db_s[...], w1c[...])).astype(BF16).astype(F32)
+        low = lax.broadcasted_iota(jnp.int32, (rows, 128), 1) < 64
+        for j in range(d_model // 128):
+            o_blk = o[:, j * 128:(j + 1) * 128]
+            r_blk = dr[:, j * 128:(j + 1) * 128]
+            back[2 * j, ep] = jnp.where(low, o_blk, pltpu.roll(r_blk, 64, 1)).astype(BF16)
+            back[2 * j + 1, ep] = jnp.where(low, pltpu.roll(o_blk, 64, 1), r_blk).astype(BF16)
+        for a in range(1, n_tp):
+            row_copy(a, b).start()
+
+        @pl.when(b > 0)
+        def _():
+            row_copy(0, b).start()
+
+        @pl.when(b == 0)
+        def _():
+            own.start()
+
+        acco[...] += dot_tn(h_s[...], d)
+        acc0[...] += dot_tn(r, da_s[...])
+        acc1[...] += dot_tn(r, db_s[...])
+        return 0
+
+    lax.fori_loop(0, n_ep, shard, 0)
+    for j in range(n_tp):
+        g0_out[j] = acc0[:, j * part:(j + 1) * part].astype(BF16)
+        g1_out[j] = acc1[:, j * part:(j + 1) * part].astype(BF16)
+    go_out[...] = acco[...].astype(BF16)
     own.wait()
-    for cp in copies:
-        cp.wait()
-
-
-def combine_kernel(pos_ref, table_ref, gate_ref, dy_ref, y_out, dr_out, dg_out, tab, c1, c2):
-    s = lax.axis_index("tp")
-    slots = table_ref.shape[0]
-    tokens = dy_ref.shape[0]
-    half = tokens // 2
-    step = 2048
-
-    def widen(i, _):
-        sl = pl.ds(pl.multiple_of(i * step, step), step)
-        tab[sl, :] = table_ref[sl, :].astype(F32)
-        return 0
-
-    lax.fori_loop(0, slots // step, widen, 0)
-    tab[pl.ds(slots, 8), :] = jnp.zeros((8, 128), F32)
-
-    unroll = 16
-
-    def look(i, _):
-        t0 = i * unroll
-        for u in range(unroll):
-            c1[pl.ds(t0 + u, 1), :] = tab[pl.ds(pos_ref[t0 + u], 1), :]
-            c2[pl.ds(t0 + u, 1), :] = tab[pl.ds(pos_ref[tokens + t0 + u], 1), :]
-        return 0
-
-    lax.fori_loop(0, tokens // unroll, look, 0)
-
-    blk = 512
-    low = lax.broadcasted_iota(jnp.int32, (blk, 128), 1) < 64
-    odd = lax.rem(s, 2) == 1
-    for i in range(half // blk):
-        pieces = []
-        for h in range(2):
-            t0 = h * half + i * blk
-            a1 = c1[t0:t0 + blk, :]
-            a2 = c2[t0:t0 + blk, :]
-            dy = dy_ref[t0:t0 + blk, :].astype(F32)
-            dy = jnp.where(odd, pltpu.roll(dy, 64, 1), dy)
-            y = gate_ref[t0:t0 + blk, 0:1] * a1 + gate_ref[t0:t0 + blk, 1:2] * a2
-            pieces.append((y, a1 + a2))
-            for k, av in enumerate((a1, a2)):
-                prod = jnp.where(low, dy * av, 0.0)
-                line = jnp.sum(prod.T, axis=0, keepdims=True)
-                row = k * 4 + t0 // 1024
-                col = t0 % 1024
-                dg_out[row:row + 1, col:col + blk] = line
-        (ya, da), (yb, db) = pieces
-        y_out[i * blk:(i + 1) * blk, :] = jnp.where(low, ya, pltpu.roll(yb, 64, 1)).astype(BF16)
-        dr_out[i * blk:(i + 1) * blk, :] = jnp.where(low, pltpu.roll(da, 64, 1), db)
-
-
-def return_kernel(n_tp, n_ep, y_ref, dr_ref, dg_ref, prob_ref, gate_ref, idx_ref, stat_ref, x_ref, wgt_ref,
-                  g0_ref, g1_ref, go_ref,
+    for b in range(n_ep):
+        for a in range(n_tp):
+            if a + b > 0:
+                row_copy(a, b).wait()
+
+
+def return_kernel(n_tp, n_ep, pos_ref, gcol_ref, dyc_ref, prob_ref, gate_ref, idx_ref, stat_ref, wgt_ref,
+                  table_ref, x_ref, g0_ref, g1_ref, go_ref,
                   gy_out, gx_out, g0_out, g1_out, go_out, dwg_out, aux_out,
+                  tab_in, tab, c1, c2, y_buf, dr_buf, dg_buf, x_buf, tab_sem,
                   dg_all, dx_buf, dl_buf, dwg_buf, dwg_all,
                   g_send, g_recv, dg_send, dg_recv, ag_send, ag_recv, wg_send, wg_recv, loc):
     s = lax.axis_index("tp")
@@ -285,13 +256,18 @@
     total_tokens = float(tokens * n_ep)
     half = tokens // 2
     copies = []
-    for p in range(1, n_tp):
-        peer = lax.rem(s + p, n_tp)
-        copies.append(remote(dg_ref, dg_all.at[s], dg_send.at[p], dg_recv.at[p], peer, q))
-        copies[-1].start()
-    dg_copies = list(copies)
-    dg_own = pltpu.make_async_copy(dg_ref, dg_all.at[s], loc.at[0])
-    dg_own.start()
+    local = []
+    grads = ((g0_ref, g0_out), (g1_ref, g1_out), (go_ref, go_out))
+
+    def send_grads(a):
+        src, dst = grads[a]
+        for p in range(1, n_tp):
+            peer = lax.rem(s + p, n_tp)
+            cp = remote(src.at[peer], dst.at[s], g_send.at[a, p], g_recv.at[a, p], peer, q)
+            cp.start()
+            copies.append(cp)
+        local.append(pltpu.make_async_copy(src.at[s], dst.at[s], loc.at[3 + a]))
+        local[-1].start()
 
     class Gather:
         def __init__(self, a, out):
@@ -389,18 +365,65 @@
 
     gat_y = Gather(0, gy_out)
     gat_x = Gather(1, gx_out)
-    gat_y.begin(y_ref)
-
-    grads = ((g0_ref, g0_out), (g1_ref, g1_out), (go_ref, go_out))
-    local = [dg_own]
-    for a, (src, dst) in enumerate(grads):
-        for p in range(1, n_tp):
-            peer = lax.rem(s + p, n_tp)
-            cp = remote(src.at[peer], dst.at[s], g_send.at[a, p], g_recv.at[a, p], peer, q)
-            cp.start()
-            copies.append(cp)
-        local.append(pltpu.make_async_copy(src.at[s], dst.at[s], loc.at[3 + a]))
-        local[-1].start()
+    slots = tab_in.shape[0] * tab_in.shape[1]
+    cap = tab_in.shape[1]
+    groups = 8
+    per = tab_in.shape[0] // groups
+    loads = [pltpu.make_async_copy(table_ref.at[pl.ds(k * per, per)], tab_in.at[pl.ds(k * per, per)], tab_sem.at[k]) for k in range(groups)]
+    for cp in loads:
+        cp.start()
+    x_load = pltpu.make_async_copy(x_ref, x_buf, loc.at[7])
+    x_load.start()
+    send_grads(0)
+
+    tab[pl.ds(slots, 8), :] = jnp.zeros((8, 128), F32)
+    for k in range(groups):
+        loads[k].wait()
+
+        def widen(i, _):
+            tab[pl.ds(pl.multiple_of((k * per + i) * cap, cap), cap), :] = tab_in[k * per + i].astype(F32)
+            return 0
+
+        lax.fori_loop(0, per, widen, 0)
+
+    unroll = 16
+
+    def look(i, _):
+        t0 = i * unroll
+        for u in range(unroll):
+            c1[pl.ds(t0 + u, 1), :] = tab[pl.ds(pos_ref[t0 + u], 1), :]
+            c2[pl.ds(t0 + u, 1), :] = tab[pl.ds(pos_ref[tokens + t0 + u], 1), :]
+        return 0
+
+    lax.fori_loop(0, tokens // unroll, look, 0)
+
+    blk = 512
+    low = lax.broadcasted_iota(jnp.int32, (blk, 128), 1) < 64
+    for i in range(half // blk):
+        pieces = []
+        for h in range(2):
+            t0 = h * half + i * blk
+            a1 = c1[t0:t0 + blk, :]
+            a2 = c2[t0:t0 + blk, :]
+            dy = dyc_ref[t0:t0 + blk, :].astype(F32)
+            pieces.append((gcol_ref[t0:t0 + blk, 0:1] * a1 + gcol_ref[t0:t0 + blk, 1:2] * a2, a1 + a2))
+            for k, av in enumerate((a1, a2)):
+                prod = jnp.where(low, dy * av, 0.0)
+                row = k * 4 + t0 // 1024
+                col = t0 % 1024
+                dg_buf[row:row + 1, col:col + blk] = jnp.sum(prod.T, axis=0, keepdims=True)
+        (ya, da), (yb, db) = pieces
+        y_buf[i * blk:(i + 1) * blk, :] = jnp.where(low, ya, pltpu.roll(yb, 64, 1)).astype(BF16)
+        dr_buf[i * blk:(i + 1) * blk, :] = jnp.where(low, pltpu.roll(da, 64, 1), db)
+
+    dg_copies = []
+    for p in range(1, n_tp):
+        peer = lax.rem(s + p, n_tp)
+        dg_copies.append(remote(dg_buf, dg_all.at[s], dg_send.at[p], dg_recv.at[p], peer, q))
+        dg_copies[-1].start()
+    dg_own = pltpu.make_async_copy(dg_buf, dg_all.at[s], loc.at[0])
+    dg_own.start()
+    gat_y.begin(y_buf)
 
     counts = stat_ref[0, :, 0:1]
     sums = stat_ref[0, :, 1:2]
@@ -442,10 +465,11 @@
     dl_all = dl_buf[...]
     xr = dot_tn(dl_all, w_top) + dot_tn(dl_all[:2 * experts], w_mid) + dot_tn(dl_all[:experts], wlo)
     xr = jnp.where(left, xr[:half], pltpu.roll(xr[half:], 64, 1))
-    dx_buf[...] = (dr_ref[...] + xr).astype(BF16)
+    dx_buf[...] = (dr_buf[...] + xr).astype(BF16)
     gat_x.begin(dx_buf)
     gat_y.relay(1)
-    dw = dot_nn(dl_all, x_ref[...])
+    x_load.wait()
+    dw = dot_nn(dl_all, x_buf[...])
     dwg_buf[...] = dw[:experts] + (dw[experts:2 * experts] + dw[2 * experts:])
     wg_copies = []
     for p in range(1, n_ep):
@@ -456,8 +480,10 @@
     wg_own.start()
     gat_y.relay(2)
     gat_x.relay(1)
+    send_grads(1)
     gat_y.relay(3)
     gat_x.relay(2)
+    send_grads(2)
     gat_x.relay(3)
     wg_own.wait()
     for cp in wg_copies:
@@ -470,9 +496,9 @@
     gat_x.finish()
     for cp in dg_copies:
         cp.wait_send()
-    for cp in local[1:]:
+    for cp in local:
         cp.wait()
-    for cp in copies[len(dg_copies):]:
+    for cp in copies:
         cp.wait()
 
 
@@ -511,55 +537,35 @@
         wgt = w_router.T
         side = pltpu.CompilerParams(has_side_effects=True, vmem_limit_bytes=VMEM_LIMIT)
 
-        rows, drows, w0, w1, wo, prob, gate, stat = pl.pallas_call(
+        rows, drows, w0, w1, wo, prob, gate, stat, dy_cols, gate_cols = pl.pallas_call(
             functools.partial(dispatch_kernel, n_tp, n_ep, cap),
             name="moe_dispatch",
             out_shape=(sds((n_ep, cap, d_model), BF16), sds((n_ep, cap, d_model), BF16),
                        sds(gelu_loc.shape, BF16), sds(lin_loc.shape, BF16), sds(out_loc.shape, BF16),
-                       sds((experts, tokens), F32), sds((8, tokens), F32), sds((n_ep, experts, 128), F32)),
-            in_specs=[vmem] * 5 + [hbm] * 3,
-            out_specs=(hbm, hbm, hbm, hbm, hbm, vmem, vmem, vmem),
-            scratch_shapes=[pltpu.VMEM((n_ep, cap, d_model), BF16), pltpu.VMEM((n_ep, cap, d_model), BF16),
+                       sds((experts, tokens), F32), sds((8, tokens), F32), sds((n_ep, experts, 128), F32),
+                       sds((tokens, 128), BF16), sds((tokens, 8), F32)),
+            in_specs=[hbm] * 2 + [vmem] * 3 + [hbm] * 3,
+            out_specs=(hbm, hbm, hbm, hbm, hbm, vmem, vmem, vmem, vmem, vmem),
+            scratch_shapes=[pltpu.VMEM((tokens, d_model), BF16), pltpu.VMEM((tokens, d_model), BF16),
+                            pltpu.VMEM((n_ep, cap, d_model), BF16), pltpu.VMEM((n_ep, cap, d_model), BF16),
                             pltpu.VMEM((experts, 128), F32), pltpu.VMEM((cap, d_model), F32), pltpu.VMEM((cap, d_model), F32),
-                            dma((3, n_tp)), dma((3, n_tp)), dma((2, n_ep)), dma((2, n_ep)), dma((n_ep,)), dma((n_ep,)), dma((6,))],
+                            dma((3, n_tp)), dma((3, n_tp)), dma((2, n_ep)), dma((2, n_ep)), dma((n_ep,)), dma((n_ep,)), dma((8,))],
             compiler_params=side,
         )(x_loc, dy_loc, idx_t, key_t, wgt, gelu_loc, lin_loc, out_loc)
 
-        full = lambda shape: pl.BlockSpec(shape, lambda i: (0,) * len(shape))
-        back, g0, g1, go = pl.pallas_call(
-            functools.partial(expert_kernel, n_tp),
+        table, g0, g1, go = pl.pallas_call(
+            functools.partial(expert_kernel, n_tp, n_ep),
             name="moe_expert",
-            grid=(n_ep,),
-            out_shape=(sds((n_tp, n_ep, cap, 128), BF16), sds((n_tp, d_model, part), BF16), sds((n_tp, d_model, part), BF16), sds((width, d_model), BF16)),
-            in_specs=[pl.BlockSpec((1, cap, d_model), lambda i: (i, 0, 0)), pl.BlockSpec((1, cap, d_model), lambda i: (i, 0, 0)),
-                      full((n_tp, d_model, part)), full((n_tp, d_model, part)), full((width, d_model))],
-            out_specs=(pl.BlockSpec((n_tp, 1, cap, 128), lambda i: (0, i, 0, 0)), full((n_tp, d_model, part)), full((n_tp, d_model, part)), full((width, d_model))),
+            out_shape=(sds((n_tp * n_ep, cap, 128), BF16), sds((n_tp, d_model, part), BF16), sds((n_tp, d_model, part), BF16), sds((width, d_model), BF16)),
+            in_specs=[vmem] * 5,
+            out_specs=(hbm, vmem, vmem, vmem),
             scratch_shapes=[pltpu.VMEM((d_model, width), BF16), pltpu.VMEM((d_model, width), BF16),
                             pltpu.VMEM((cap, width), BF16), pltpu.VMEM((cap, width), BF16), pltpu.VMEM((cap, width), BF16),
-                            pltpu.VMEM((d_model, width), F32), pltpu.VMEM((d_model, width), F32), pltpu.VMEM((width, d_model), F32)],
-            compiler_params=pltpu.CompilerParams(dimension_semantics=("arbitrary",), vmem_limit_bytes=VMEM_LIMIT),
+                            pltpu.VMEM((d_model, width), F32), pltpu.VMEM((d_model, width), F32), pltpu.VMEM((width, d_model), F32),
+                            pltpu.VMEM((n_tp, n_ep, cap, 128), BF16),
+                            dma((n_tp, n_ep)), dma((n_tp, n_ep)), dma(())],
+            compiler_params=side,
         )(rows, drows, w0, w1, wo.reshape(width, d_model))
-
-        table = pl.pallas_call(
-            functools.partial(exchange_kernel, n_tp, n_ep),
-            name="moe_exchange",
-            out_shape=sds((n_tp * n_ep, cap, 128), BF16),
-            in_specs=[hbm],
-            out_specs=hbm,
-            scratch_shapes=[dma((n_tp, n_ep)), dma((n_tp, n_ep)), dma(())],
-            compiler_params=side,
-        )(back)
-
-        dy_cols = lax.dynamic_slice_in_dim(dy_loc, (s // 2) * 128, 128, axis=1)
-        y_pk, dr_pk, dg = pl.pallas_call(
-            combine_kernel,
-            name="moe_combine",
-            out_shape=(sds((tokens // 2, 128), BF16), sds((tokens // 2, 128), F32), sds((8, tokens // 4), F32)),
-            in_specs=[pl.BlockSpec(memory_space=pltpu.SMEM), vmem, vmem, vmem],
-            out_specs=(vmem, vmem, vmem),
-            scratch_shapes=[pltpu.VMEM((slots + 8, 128), F32), pltpu.VMEM((tokens, 128), F32), pltpu.VMEM((tokens, 128), F32)],
-            compiler_params=pltpu.CompilerParams(vmem_limit_bytes=VMEM_LIMIT),
-        )(pos, table.reshape(slots, 128), gate[:2].T, dy_cols)
 
         col0 = s * (d_model // n_tp)
         wg_cols = jnp.pad(lax.dynamic_slice_in_dim(wgt, col0, d_model // n_tp, axis=1), ((0, 0), (0, 64)))
@@ -569,14 +575,18 @@
             out_shape=(sds((n_tp, tokens // 2, 128), BF16), sds((n_tp, tokens // 2, 128), BF16),
                        sds(gelu_loc.shape, BF16), sds(lin_loc.shape, BF16), sds(out_loc.shape, BF16),
                        sds((experts, d_model), F32), sds((8, 128), F32)),
-            in_specs=[vmem] * 9 + [hbm] * 3,
+            in_specs=[pl.BlockSpec(memory_space=pltpu.SMEM)] + [vmem] * 7 + [hbm] * 5,
             out_specs=(hbm, hbm, hbm, hbm, hbm, vmem, vmem),
-            scratch_shapes=[pltpu.VMEM((n_tp, 8, tokens // 4), F32), pltpu.VMEM((tokens // 2, 128), BF16),
+            scratch_shapes=[pltpu.VMEM((n_tp * n_ep, cap, 128), BF16), pltpu.VMEM((slots + 8, 128), F32),
+                            pltpu.VMEM((tokens, 128), F32), pltpu.VMEM((tokens, 128), F32),
+                            pltpu.VMEM((tokens // 2, 128), BF16), pltpu.VMEM((tokens // 2, 128), F32), pltpu.VMEM((8, tokens // 4), F32),
+                            pltpu.VMEM((tokens, d_model), BF16), dma((8,)),
+                            pltpu.VMEM((n_tp, 8, tokens // 4), F32), pltpu.VMEM((tokens // 2, 128), BF16),
                             pltpu.VMEM((3 * experts, tokens), BF16), pltpu.VMEM((experts, d_model), F32), pltpu.VMEM((n_ep, experts, d_model), F32),
                             dma((3, n_tp)), dma((3, n_tp)), dma((n_tp,)), dma((n_tp,)),
-                            dma((2, n_tp, 3)), dma((2, n_tp)), dma((n_ep,)), dma((n_ep,)), dma((7,))],
+                            dma((2, n_tp, 3)), dma((2, n_tp)), dma((n_ep,)), dma((n_ep,)), dma((8,))],
             compiler_params=side,
-        )(y_pk, dr_pk, dg, prob, gate, idx_t, stat, x_loc, wg_cols, g0, g1, go.reshape(out_loc.shape))
+        )(pos, gate_cols, dy_cols, prob, gate, idx_t, stat, wg_cols, table, x_loc, g0, g1, go.reshape(out_loc.shape))
 
         pair = pl.BlockSpec((2, tokens // 2, 128), lambda j: (j, 0, 0))
         cols = pl.BlockSpec((tokens, 128), lambda j: (0, j))

time: 419 us -> 361 us (0.86)
  Pallas kernels: 403 us -> 350 us
  local copies, waits for them, and re-layouts: 13.3 us -> 8.15 us
    pallas_call x1, Pallas kernels: 191 us -> 159 us  [device_step(): pl.pallas_call(functools.partial(return_kernel, n_tp, n_ep), name='moe_re...]
    pallas_call x3 -> x1, Pallas kernels: 129 us -> 109 us  [device_step(): pl.pallas_call(functools.partial(expert_kernel, n_tp, n_ep), name='moe_ex...]
where the time goes in v2:
time: 361 us
  Pallas kernels  350 us (97%)
  local copies, waits for them, and re-layouts  8.15 us (2%)
    pallas_call x1, Pallas kernels, device_step(): pl.pallas_call(functools.partial(return_kernel, n_tp, n_ep), name='moe_re...  159 us
    pallas_call x1, Pallas kernels, device_step(): pl.pallas_call(functools.partial(expert_kernel, n_tp, n_ep), name='moe_ex...  109 us
    pallas_call x1, Pallas kernels, device_step(): pl.pallas_call(functools.partial(dispatch_kernel, n_tp, n_ep, cap), name=...  74.6 us
    pallas_call x1, Pallas kernels, device_step(): pl.pallas_call(interleave_kernel, name='moe_interleave', grid=(n_tp // 2,...  7.63 us

profile of v2, /device:TPU:0, one launch (start us, length us, event | category | flops | bytes accessed | tf_op | source)
XLA Modules:
  0.0 360.6 jit_solution(16528069039441938027)
XLA Ops:
  0.6 0.8 dynamic-slice_bitcast_fusion
  1.4 0.6 pad.4.wgt_ref
  2.0 1.5 fusion.4
  3.6 0.6 copy.15
  4.2 74.6 %moe_dispatch.1 = (bf16[4,512,512]{2,1,0:T(8,128)(2,1)}, bf16[4,512,512]{2,1,0:T(8,128)(2,1)}, bf16[8,512,128]{2,1,0:T(8,128)(2,1)}, bf16[8,512,128]{2,1,0:T(8,1...) custom-call(bf16[4096,512]{1,0:T(8,128)(2,1)} %x_ref.3, ...), custom_call_target="tpu_custom_call" | custom-call | tf_op jit(solution)/shard_map/moe_dispatch/pallas_call | solution.py:540
  78.8 108.8 %moe_expert.1 = (bf16[32,512,128]{2,1,0:T(8,128)(2,1)}, bf16[8,512,128]{2,1,0:T(8,128)(2,1)}, bf16[8,512,128]{2,1,0:T(8,128)(2,1)}, bf16[1024,512]{1,0:T(8,128)(2,1)}) custom-call(bf16[4,512,512]{2,1,0:T(8,128)(2,1)} %get-tuple-element.35.r_ref, bf16[4,512,512]{2,1,0:T(8,128)(2,1)} %get-tuple-element.36.d_ref, ...), custom_call_target="tpu_custom_call" | custom-call | tf_op jit(solution)/shard_map/moe_expert/pallas_call | solution.py:556
  187.7 159.1 %moe_return.1 = (bf16[8,2048,128]{2,1,0:T(8,128)(2,1)}, bf16[8,2048,128]{2,1,0:T(8,128)(2,1)}, bf16[8,512,128]{2,1,0:T(8,128)(2,1)}, bf16[8,512,128]{2,1,0:T(8,1...) custom-call(s32[8192]{0:T(1024)} %bitcast.31, f32[4096,8]{1,0:T(8,128)} %get-tuple-element.30.gcol_ref, ...), custom_call_target="tpu_custom_call" | custom-call | tf_op jit(solution)/shard_map/moe_return/pallas_call | solution.py:572
  346.8 1.2 slice.3
  348.0 0.0 copy-start.1
  348.0 7.6 %moe_interleave.1 = (bf16[4096,512]{1,0:T(8,128)(2,1)}, bf16[4096,512]{1,0:T(8,128)(2,1)}) custom-call(bf16[8,2048,128]{2,1,0:T(8,128)(2,1)} %get-tuple-element.44.gy_ref, bf16[8,2048,128]{2,1,0:T(8,128)(2,1)} %get-tuple-element.45.gx_ref), custom_call_target="tpu_custom_call" | custom-call | tf_op jit(solution)/shard_map/moe_interleave/pallas_call | solution.py:593
  355.6 0.0 copy-start
  355.6 0.0 copy-start.2
  355.6 2.4 copy.20
  358.0 0.0 copy-done.1
  358.0 1.0 copy.21
  359.0 0.0 copy-done
  359.0 1.0 copy.22
  360.0 0.0 copy-done.2
  360.0 0.6 copy.23
Async XLA Ops:
  348.0 10.0 %copy-start.1 = (bf16[8,512,128]{2,1,0:T(8,128)(2,1)S(1)}, bf16[8,512,128]{2,1,0:T(8,128)(2,1)}, u32[]{:S(2)}) copy-start(bf16[8,512,128]{2,1,0:T(8,128)(2,1)} %get-tuple-element.65) | copy-start | bytes 3145732
  355.6 3.3 copy-start
  355.6 4.3 %copy-start.2 = (f32[32,512]{1,0:T(8,128)S(1)}, f32[32,512]{1,0:T(8,128)}, u32[]{:S(2)}) copy-start(f32[32,512]{1,0:T(8,128)} %get-tuple-element.51) | copy-start | bytes 196612

commit v3 on v2

--- a/solution.py
+++ b/solution.py
@@ -164,8 +164,8 @@
         cp.wait()
 
 
-def expert_kernel(n_tp, n_ep, r_ref, d_ref, w0_ref, w1_ref, wo_ref, table_out, g0_out, g1_out, go_out,
-                  w0c, w1c, h_s, da_s, db_s, acc0, acc1, acco, back, send, recv, loc):
+def expert_kernel(n_tp, n_ep, r_ref, d_ref, w0_ref, w1_ref, wo_ref, table_out, g0_out, g1_out, go_out, p0_out, p1_out, po_out,
+                  w0c, w1c, h_s, da_s, db_s, acc0, acc1, acco, back, send, recv, loc, p_send, p_recv):
     s = lax.axis_index("tp")
     q = lax.axis_index("ep")
     me = s * n_ep + q
@@ -232,20 +232,29 @@
     for j in range(n_tp):
         g0_out[j] = acc0[:, j * part:(j + 1) * part].astype(BF16)
         g1_out[j] = acc1[:, j * part:(j + 1) * part].astype(BF16)
-    go_out[...] = acco[...].astype(BF16)
+    for j in range(n_tp):
+        go_out[j] = acco[j * part:(j + 1) * part, :].astype(BF16)
+    y = lax.rem(s, 2)
+    crossing = []
+    for a, (src, dst) in enumerate(((g0_out, p0_out), (g1_out, p1_out), (go_out, po_out))):
+        for k in range(n_tp // 2):
+            crossing.append(remote(src.at[2 * k + 1 - y], dst.at[k], p_send.at[a, k], p_recv.at[a, k], s + 1 - 2 * y, q))
+            crossing[-1].start()
     own.wait()
     for b in range(n_ep):
         for a in range(n_tp):
             if a + b > 0:
                 row_copy(a, b).wait()
+    for cp in crossing:
+        cp.wait()
 
 
 def return_kernel(n_tp, n_ep, pos_ref, gcol_ref, dyc_ref, prob_ref, gate_ref, idx_ref, stat_ref, wgt_ref,
-                  table_ref, x_ref, g0_ref, g1_ref, go_ref,
+                  table_ref, x_ref, g0_ref, g1_ref, go_ref, p0_ref, p1_ref, po_ref,
                   gy_out, gx_out, g0_out, g1_out, go_out, dwg_out, aux_out,
                   tab_in, tab, c1, c2, y_buf, dr_buf, dg_buf, x_buf, tab_sem,
                   dg_all, dx_buf, dl_buf, dwg_buf, dwg_all,
-                  g_send, g_recv, dg_send, dg_recv, ag_send, ag_recv, wg_send, wg_recv, loc):
+                  stay_w, stay_o, g_send, g_recv, g_loc, dg_send, dg_recv, ag_send, ag_recv, ag_loc, wg_send, wg_recv, loc):
     s = lax.axis_index("tp")
     q = lax.axis_index("ep")
     n_z = n_tp // 2
@@ -257,24 +266,38 @@
     half = tokens // 2
     copies = []
     local = []
-    grads = ((g0_ref, g0_out), (g1_ref, g1_out), (go_ref, go_out))
-
-    def send_grads(a):
-        src, dst = grads[a]
-        for p in range(1, n_tp):
-            peer = lax.rem(s + p, n_tp)
-            cp = remote(src.at[peer], dst.at[s], g_send.at[a, p], g_recv.at[a, p], peer, q)
+    grads = ((g0_ref, p0_ref, g0_out), (g1_ref, p1_ref, g1_out), (go_ref, po_ref, go_out))
+    queue = [(a, h, p) for a in range(3) for p in range(1, n_z) for h in range(2)]
+
+    def send_grads(n):
+        for _ in range(min(n, len(queue))):
+            a, h, p = queue.pop(0)
+            own, other, dst = grads[a]
+            k = lax.rem(z + p, n_z)
+            src = other.at[k] if h else own.at[2 * k + y]
+            source = s + 1 - 2 * y if h else s
+            cp = remote(src, dst.at[source], g_send.at[a, h, p], g_recv.at[a, h, p], 2 * k + y, q)
             cp.start()
             copies.append(cp)
-        local.append(pltpu.make_async_copy(src.at[s], dst.at[s], loc.at[3 + a]))
-        local[-1].start()
+
+    stay_in, stay_out = [], []
+    for a, (own, other, dst) in enumerate(grads):
+        for h, (src, source) in enumerate(((own.at[s], s), (other.at[z], s + 1 - 2 * y))):
+            mid = stay_o.at[h] if a == 2 else stay_w.at[a, h]
+            stay_in.append(pltpu.make_async_copy(src, mid, g_loc.at[a, h]))
+            stay_out.append(pltpu.make_async_copy(mid, dst.at[source], g_loc.at[a, 2 + h]))
+    for cp in stay_in:
+        cp.start()
 
     class Gather:
-        def __init__(self, a, out):
-            self.a, self.out = a, out
+        def __init__(self, a, out, rows):
+            self.a, self.out, self.rows = a, out, rows
+
+        def blk(self, owner):
+            return self.out.at[owner, self.rows]
 
         def hop(self, src, owner, way, tp):
-            return remote(src, self.out.at[owner], ag_send.at[self.a, owner, way], ag_recv.at[self.a, owner], tp, q)
+            return remote(src, self.blk(owner), ag_send.at[self.a, owner, way], ag_recv.at[self.a, owner], tp, q)
 
         def up(self, src, owner):
             return self.hop(src, owner, 0, lax.rem(s + 2, n_tp))
@@ -286,8 +309,9 @@
             return self.hop(src, owner, 2, s + 1 - 2 * y)
 
         def begin(self, src):
+            src = src.at[self.rows]
             self.src = src
-            self.own = pltpu.make_async_copy(src, self.out.at[s], loc.at[1 + self.a])
+            self.own = pltpu.make_async_copy(src, self.blk(s), ag_loc.at[self.a])
 
             @pl.when(z < n_z - 1)
             def _():
@@ -304,7 +328,7 @@
             @pl.when(z >= dist)
             def _():
                 owner = lax.rem(s + n_tp - 2 * dist, n_tp)
-                blk = self.out.at[owner]
+                blk = self.blk(owner)
                 self.up(blk, owner).wait_recv()
 
                 @pl.when(z < n_z - 1)
@@ -316,7 +340,7 @@
             @pl.when(z + dist < n_z)
             def _():
                 owner = lax.rem(s + 2 * dist, n_tp)
-                blk = self.out.at[owner]
+                blk = self.blk(owner)
                 self.down(blk, owner).wait_recv()
 
                 @pl.when(z > 0)
@@ -340,7 +364,7 @@
                 @pl.when(z >= dist)
                 def _():
                     owner = lax.rem(s + n_tp - 2 * dist, n_tp)
-                    blk = self.out.at[owner]
+                    blk = self.blk(owner)
 
                     @pl.when(z < n_z - 1)
                     def _():
@@ -351,7 +375,7 @@
                 @pl.when(z + dist < n_z)
                 def _():
                     owner = lax.rem(s + 2 * dist, n_tp)
-                    blk = self.out.at[owner]
+                    blk = self.blk(owner)
 
                     @pl.when(z > 0)
                     def _():
@@ -361,10 +385,11 @@
 
             for k in range(n_z):
                 owner = 2 * k + 1 - y
-                self.across(self.out.at[owner], owner).wait_recv()
-
-    gat_y = Gather(0, gy_out)
-    gat_x = Gather(1, gx_out)
+                self.across(self.blk(owner), owner).wait_recv()
+
+    quarter = half // 2
+    gat_y = [Gather(h, gy_out, pl.ds(h * quarter, quarter)) for h in range(2)]
+    gat_x = [Gather(2 + h, gx_out, pl.ds(h * quarter, quarter)) for h in range(2)]
     slots = tab_in.shape[0] * tab_in.shape[1]
     cap = tab_in.shape[1]
     groups = 8
@@ -374,7 +399,7 @@
         cp.start()
     x_load = pltpu.make_async_copy(x_ref, x_buf, loc.at[7])
     x_load.start()
-    send_grads(0)
+    send_grads(6)
 
     tab[pl.ds(slots, 8), :] = jnp.zeros((8, 128), F32)
     for k in range(groups):
@@ -395,27 +420,34 @@
             c2[pl.ds(t0 + u, 1), :] = tab[pl.ds(pos_ref[tokens + t0 + u], 1), :]
         return 0
 
-    lax.fori_loop(0, tokens // unroll, look, 0)
-
     blk = 512
     low = lax.broadcasted_iota(jnp.int32, (blk, 128), 1) < 64
-    for i in range(half // blk):
-        pieces = []
+    for part in range(2):
         for h in range(2):
-            t0 = h * half + i * blk
-            a1 = c1[t0:t0 + blk, :]
-            a2 = c2[t0:t0 + blk, :]
-            dy = dyc_ref[t0:t0 + blk, :].astype(F32)
-            pieces.append((gcol_ref[t0:t0 + blk, 0:1] * a1 + gcol_ref[t0:t0 + blk, 1:2] * a2, a1 + a2))
-            for k, av in enumerate((a1, a2)):
-                prod = jnp.where(low, dy * av, 0.0)
-                row = k * 4 + t0 // 1024
+            first = (h * half + part * quarter) // unroll
+            lax.fori_loop(first, first + quarter // unroll, look, 0)
+        for i in range(part * quarter // blk, (part + 1) * quarter // blk):
+            pieces = []
+            for h in range(2):
+                t0 = h * half + i * blk
+                a1 = c1[t0:t0 + blk, :]
+                a2 = c2[t0:t0 + blk, :]
+                dy = dyc_ref[t0:t0 + blk, :].astype(F32)
+                pieces.append((gcol_ref[t0:t0 + blk, 0:1] * a1 + gcol_ref[t0:t0 + blk, 1:2] * a2, a1 + a2))
+                prod = jnp.where(low, dy * a1, pltpu.roll(dy * a2, 64, 1)).T
+                row = t0 // 1024
                 col = t0 % 1024
-                dg_buf[row:row + 1, col:col + blk] = jnp.sum(prod.T, axis=0, keepdims=True)
-        (ya, da), (yb, db) = pieces
-        y_buf[i * blk:(i + 1) * blk, :] = jnp.where(low, ya, pltpu.roll(yb, 64, 1)).astype(BF16)
-        dr_buf[i * blk:(i + 1) * blk, :] = jnp.where(low, pltpu.roll(da, 64, 1), db)
-
+                dg_buf[row:row + 1, col:col + blk] = jnp.sum(prod[:64], axis=0, keepdims=True)
+                dg_buf[4 + row:5 + row, col:col + blk] = jnp.sum(prod[64:], axis=0, keepdims=True)
+            (ya, da), (yb, db) = pieces
+            y_buf[i * blk:(i + 1) * blk, :] = jnp.where(low, ya, pltpu.roll(yb, 64, 1)).astype(BF16)
+            dr_buf[i * blk:(i + 1) * blk, :] = jnp.where(low, pltpu.roll(da, 64, 1), db)
+        gat_y[part].begin(y_buf)
+
+    for cin, cout in zip(stay_in, stay_out):
+        cin.wait()
+        cout.start()
+    local.extend(stay_out)
     dg_copies = []
     for p in range(1, n_tp):
         peer = lax.rem(s + p, n_tp)
@@ -423,14 +455,14 @@
         dg_copies[-1].start()
     dg_own = pltpu.make_async_copy(dg_buf, dg_all.at[s], loc.at[0])
     dg_own.start()
-    gat_y.begin(y_buf)
+    gat_y[0].relay(1)
 
     counts = stat_ref[0, :, 0:1]
     sums = stat_ref[0, :, 1:2]
     for e in range(1, n_ep):
         counts = counts + stat_ref[e, :, 0:1]
         sums = sums + stat_ref[e, :, 1:2]
-    aux_out[...] = jnp.broadcast_to(jnp.sum(counts * sums, axis=0, keepdims=True) * (experts / (total_tokens * total_tokens)), aux_out.shape)
+    aux_out[0, 0] = jnp.sum(counts * sums) * (experts / (total_tokens * total_tokens))
     aux_cot = counts * (AUX_WEIGHT * experts / (total_tokens * total_tokens))
     for cp in dg_copies:
         cp.wait_recv()
@@ -458,7 +490,10 @@
         dl_buf[experts:2 * experts, cols] = mid
         dl_buf[2 * experts:, cols] = lo
 
-    whi, wmid, wlo = split3(wgt_ref[...])
+    wcols = wgt_ref[:, pl.ds(pl.multiple_of((s // 2) * 128, 128), 128)]
+    wcols = jnp.where(y == 1, pltpu.roll(wcols, 64, 1), wcols)
+    wcols = jnp.where(lax.broadcasted_iota(jnp.int32, wcols.shape, 1) < 64, wcols, 0.0)
+    whi, wmid, wlo = split3(wcols)
     left = lax.broadcasted_iota(jnp.int32, (half, 128), 1) < 64
     w_top = jnp.concatenate([whi, whi, whi], axis=0)
     w_mid = jnp.concatenate([wmid, wmid], axis=0)
@@ -466,8 +501,9 @@
     xr = dot_tn(dl_all, w_top) + dot_tn(dl_all[:2 * experts], w_mid) + dot_tn(dl_all[:experts], wlo)
     xr = jnp.where(left, xr[:half], pltpu.roll(xr[half:], 64, 1))
     dx_buf[...] = (dr_buf[...] + xr).astype(BF16)
-    gat_x.begin(dx_buf)
-    gat_y.relay(1)
+    gat_x[0].begin(dx_buf)
+    gat_x[1].begin(dx_buf)
+    gat_y[1].relay(1)
     x_load.wait()
     dw = dot_nn(dl_all, x_buf[...])
     dwg_buf[...] = dw[:experts] + (dw[experts:2 * experts] + dw[2 * experts:])
@@ -478,13 +514,20 @@
         wg_copies.append(cp)
     wg_own = pltpu.make_async_copy(dwg_buf, dwg_all.at[q], loc.at[6])
     wg_own.start()
-    gat_y.relay(2)
-    gat_x.relay(1)
-    send_grads(1)
-    gat_y.relay(3)
-    gat_x.relay(2)
-    send_grads(2)
-    gat_x.relay(3)
+    gat_y[0].relay(2)
+    gat_y[1].relay(2)
+    gat_x[0].relay(1)
+    gat_y[0].relay(3)
+    gat_x[1].relay(1)
+    gat_y[1].relay(3)
+    send_grads(3)
+    gat_x[0].relay(2)
+    send_grads(3)
+    gat_x[1].relay(2)
+    send_grads(3)
+    gat_x[0].relay(3)
+    gat_x[1].relay(3)
+    send_grads(3)
     wg_own.wait()
     for cp in wg_copies:
         cp.wait()
@@ -492,8 +535,8 @@
     for e in range(1, n_ep):
         tot = tot + dwg_all[e]
     dwg_out[...] = tot
-    gat_y.finish()
-    gat_x.finish()
+    for gat in gat_y + gat_x:
+        gat.finish()
     for cp in dg_copies:
         cp.wait_send()
     for cp in local:
@@ -502,7 +545,7 @@
         cp.wait()
 
 
-def interleave_kernel(gy_ref, gx_ref, y_out, dx_out):
+def interleave_kernel(gy_ref, gx_ref, g0_ref, g1_ref, go_ref, y_out, dx_out, g0_out, g1_out, go_out):
     half = gy_ref.shape[1]
     low = lax.broadcasted_iota(jnp.int32, (half, 128), 1) < 64
     for src, dst in ((gy_ref, y_out), (gx_ref, dx_out)):
@@ -510,6 +553,9 @@
         b = src[1].astype(F32)
         dst[0:half, :] = jnp.where(low, a, pltpu.roll(b, 64, 1)).astype(BF16)
         dst[half:2 * half, :] = jnp.where(low, pltpu.roll(a, 64, 1), b).astype(BF16)
+    g0_out[...] = g0_ref[...]
+    g1_out[...] = g1_ref[...]
+    go_out[...] = go_ref[...]
 
 
 def solution(mesh):
@@ -553,53 +599,55 @@
             compiler_params=side,
         )(x_loc, dy_loc, idx_t, key_t, wgt, gelu_loc, lin_loc, out_loc)
 
-        table, g0, g1, go = pl.pallas_call(
+        half_shape = lambda ref: sds((n_tp // 2,) + ref.shape[1:], BF16)
+        table, g0, g1, go, p0, p1, po = pl.pallas_call(
             functools.partial(expert_kernel, n_tp, n_ep),
             name="moe_expert",
-            out_shape=(sds((n_tp * n_ep, cap, 128), BF16), sds((n_tp, d_model, part), BF16), sds((n_tp, d_model, part), BF16), sds((width, d_model), BF16)),
+            out_shape=(sds((n_tp * n_ep, cap, 128), BF16), sds(gelu_loc.shape, BF16), sds(lin_loc.shape, BF16), sds(out_loc.shape, BF16),
+                       half_shape(gelu_loc), half_shape(lin_loc), half_shape(out_loc)),
             in_specs=[vmem] * 5,
-            out_specs=(hbm, vmem, vmem, vmem),
+            out_specs=(hbm, vmem, vmem, vmem, hbm, hbm, hbm),
             scratch_shapes=[pltpu.VMEM((d_model, width), BF16), pltpu.VMEM((d_model, width), BF16),
                             pltpu.VMEM((cap, width), BF16), pltpu.VMEM((cap, width), BF16), pltpu.VMEM((cap, width), BF16),
                             pltpu.VMEM((d_model, width), F32), pltpu.VMEM((d_model, width), F32), pltpu.VMEM((width, d_model), F32),
                             pltpu.VMEM((n_tp, n_ep, cap, 128), BF16),
-                            dma((n_tp, n_ep)), dma((n_tp, n_ep)), dma(())],
+                            dma((n_tp, n_ep)), dma((n_tp, n_ep)), dma(()), dma((3, n_tp // 2)), dma((3, n_tp // 2))],
             compiler_params=side,
         )(rows, drows, w0, w1, wo.reshape(width, d_model))
 
-        col0 = s * (d_model // n_tp)
-        wg_cols = jnp.pad(lax.dynamic_slice_in_dim(wgt, col0, d_model // n_tp, axis=1), ((0, 0), (0, 64)))
         gy, gx, grad_gelu, grad_lin, grad_out, dwg_t, aux = pl.pallas_call(
             functools.partial(return_kernel, n_tp, n_ep),
             name="moe_return",
             out_shape=(sds((n_tp, tokens // 2, 128), BF16), sds((n_tp, tokens // 2, 128), BF16),
                        sds(gelu_loc.shape, BF16), sds(lin_loc.shape, BF16), sds(out_loc.shape, BF16),
-                       sds((experts, d_model), F32), sds((8, 128), F32)),
-            in_specs=[pl.BlockSpec(memory_space=pltpu.SMEM)] + [vmem] * 7 + [hbm] * 5,
-            out_specs=(hbm, hbm, hbm, hbm, hbm, vmem, vmem),
+                       sds((experts, d_model), F32), sds((1, 1), F32)),
+            in_specs=[pl.BlockSpec(memory_space=pltpu.SMEM)] + [vmem] * 7 + [hbm] * 8,
+            out_specs=(hbm, hbm, hbm, hbm, hbm, vmem, pl.BlockSpec(memory_space=pltpu.SMEM)),
             scratch_shapes=[pltpu.VMEM((n_tp * n_ep, cap, 128), BF16), pltpu.VMEM((slots + 8, 128), F32),
                             pltpu.VMEM((tokens, 128), F32), pltpu.VMEM((tokens, 128), F32),
                             pltpu.VMEM((tokens // 2, 128), BF16), pltpu.VMEM((tokens // 2, 128), F32), pltpu.VMEM((8, tokens // 4), F32),
                             pltpu.VMEM((tokens, d_model), BF16), dma((8,)),
                             pltpu.VMEM((n_tp, 8, tokens // 4), F32), pltpu.VMEM((tokens // 2, 128), BF16),
                             pltpu.VMEM((3 * experts, tokens), BF16), pltpu.VMEM((experts, d_model), F32), pltpu.VMEM((n_ep, experts, d_model), F32),
-                            dma((3, n_tp)), dma((3, n_tp)), dma((n_tp,)), dma((n_tp,)),
-                            dma((2, n_tp, 3)), dma((2, n_tp)), dma((n_ep,)), dma((n_ep,)), dma((8,))],
+                            pltpu.VMEM((2, 2, d_model, part), BF16), pltpu.VMEM((2, part, d_model), BF16),
+                            dma((3, 2, n_tp // 2)), dma((3, 2, n_tp // 2)), dma((3, 4)), dma((n_tp,)), dma((n_tp,)),
+                            dma((4, n_tp, 3)), dma((4, n_tp)), dma((4,)), dma((n_ep,)), dma((n_ep,)), dma((8,))],
             compiler_params=side,
-        )(pos, gate_cols, dy_cols, prob, gate, idx_t, stat, wg_cols, table, x_loc, g0, g1, go.reshape(out_loc.shape))
+        )(pos, gate_cols, dy_cols, prob, gate, idx_t, stat, wgt, table, x_loc, g0, g1, go, p0, p1, po)
 
         pair = pl.BlockSpec((2, tokens // 2, 128), lambda j: (j, 0, 0))
         cols = pl.BlockSpec((tokens, 128), lambda j: (0, j))
-        y_loc, dx_loc = pl.pallas_call(
+        block = lambda ref: pl.BlockSpec((2,) + ref.shape[1:], lambda j: (j, 0, 0))
+        y_loc, dx_loc, grad_gelu, grad_lin, grad_out = pl.pallas_call(
             interleave_kernel,
             name="moe_interleave",
             grid=(n_tp // 2,),
-            out_shape=(sds((tokens, d_model), BF16), sds((tokens, d_model), BF16)),
-            in_specs=[pair, pair],
-            out_specs=(cols, cols),
+            out_shape=(sds((tokens, d_model), BF16), sds((tokens, d_model), BF16), sds(gelu_loc.shape, BF16), sds(lin_loc.shape, BF16), sds(out_loc.shape, BF16)),
+            in_specs=[pair, pair, block(gelu_loc), block(lin_loc), block(out_loc)],
+            out_specs=(cols, cols, block(gelu_loc), block(lin_loc), block(out_loc)),
             compiler_params=pltpu.CompilerParams(dimension_semantics=("arbitrary",), vmem_limit_bytes=VMEM_LIMIT),
-        )(gy, gx)
-        return y_loc, dx_loc, grad_gelu, grad_lin, grad_out, dwg_t.T, aux[0, 0]
+        )(gy, gx, grad_gelu, grad_lin, grad_out)
+        return y_loc, dx_loc, grad_gelu, grad_lin, grad_out, dwg_t.T, aux.reshape(())
 
     rows_spec = P("ep", None)
     weight_in = P("ep", None, "tp")

time: 361 us -> 347 us (0.961)
  Pallas kernels: 350 us -> 342 us
  local copies, waits for them, and re-layouts: 8.15 us -> 1.25 us
    pallas_call x1, Pallas kernels: 159 us -> 149 us  [device_step(): pl.pallas_call(functools.partial(return_kernel, n_tp, n_ep), name='moe_re...]
    unnamed x11 -> x4, local copies, waits for them, and re-layouts: 5.56 us -> 1.25 us
where the time goes in v3:
time: 347 us
  Pallas kernels  342 us (99%)
    pallas_call x1, Pallas kernels, device_step(): pl.pallas_call(functools.partial(return_kernel, n_tp, n_ep), name='moe_re...  149 us
    pallas_call x1, Pallas kernels, device_step(): pl.pallas_call(functools.partial(expert_kernel, n_tp, n_ep), name='moe_ex...  109 us
    pallas_call x1, Pallas kernels, device_step(): pl.pallas_call(functools.partial(dispatch_kernel, n_tp, n_ep, cap), name=...  74.7 us
    pallas_call x1, Pallas kernels, device_step(): pl.pallas_call(interleave_kernel, name='moe_interleave', grid=(n_tp // 2,...  9.2 us

profile of v3, /device:TPU:0, one launch (start us, length us, event | category | flops | bytes accessed | tf_op | source)
XLA Modules:
  0.0 346.9 jit_solution(17336881661875102968)
XLA Ops:
  0.6 1.5 fusion.4
  2.2 0.6 copy.15
  2.8 74.7 %moe_dispatch.1 = (bf16[4,512,512]{2,1,0:T(8,128)(2,1)}, bf16[4,512,512]{2,1,0:T(8,128)(2,1)}, bf16[8,512,128]{2,1,0:T(8,128)(2,1)}, bf16[8,512,128]{2,1,0:T(8,1...) custom-call(bf16[4096,512]{1,0:T(8,128)(2,1)} %x_ref.3, ...), custom_call_target="tpu_custom_call" | custom-call | tf_op jit(solution)/shard_map/moe_dispatch/pallas_call | solution.py:586
  77.4 109.2 %moe_expert.1 = (bf16[32,512,128]{2,1,0:T(8,128)(2,1)}, bf16[8,512,128]{2,1,0:T(8,128)(2,1)}, bf16[8,512,128]{2,1,0:T(8,128)(2,1)}, bf16[8,128,512]{2,1,0:T(8,12...) custom-call(bf16[4,512,512]{2,1,0:T(8,128)(2,1)} %get-tuple-element.41.r_ref, ...), custom_call_target="tpu_custom_call" | custom-call | tf_op jit(solution)/shard_map/moe_expert/pallas_call | solution.py:603
  186.7 148.6 %moe_return.1 = (bf16[8,2048,128]{2,1,0:T(8,128)(2,1)}, bf16[8,2048,128]{2,1,0:T(8,128)(2,1)}, bf16[8,512,128]{2,1,0:T(8,128)(2,1)}, bf16[8,512,128]{2,1,0:T(8,1...) custom-call(s32[8192]{0:T(1024)} %bitcast.29, f32[4096,8]{1,0:T(8,128)} %get-tuple-element.36.gcol_ref, ...), custom_call_target="tpu_custom_call" | custom-call | tf_op jit(solution)/shard_map/moe_return/pallas_call | solution.py:618
  335.3 0.0 copy-start
  335.3 9.2 %moe_interleave.1 = (bf16[4096,512]{1,0:T(8,128)(2,1)}, bf16[4096,512]{1,0:T(8,128)(2,1)}, bf16[8,512,128]{2,1,0:T(8,128)(2,1)}, bf16[8,512,128]{2,1,0:T(8,128)(2,1)}, bf16[8,128,512]{2,1,0:T(8,128)(2,1)}) custom-call(bf16[8,2048,128]{2,1,0:T(8,128)(2,1)} %get-tuple-element.53.gy_ref, bf16[8,2048,128]{2,1,0:T(8,128)(2,1)} %get-tuple-element.54.gx_ref, ...), custom_call_target="tpu_custom_call" | custom-call | tf_op jit(solution)/shard_map/moe_interleave/pallas_call | solution.py:641
  344.5 0.0 copy-done
  344.5 0.6 copy.18
Async XLA Ops:
  335.3 9.2 %copy-start = (f32[32,512]{1,0:T(8,128)S(1)}, f32[32,512]{1,0:T(8,128)}, u32[]{:S(2)}) copy-start(f32[32,512]{1,0:T(8,128)} %get-tuple-element.63) | copy-start | bytes 196612

commit v4 on v3

--- a/solution.py
+++ b/solution.py
@@ -164,8 +164,8 @@
         cp.wait()
 
 
-def expert_kernel(n_tp, n_ep, r_ref, d_ref, w0_ref, w1_ref, wo_ref, table_out, g0_out, g1_out, go_out, p0_out, p1_out, po_out,
-                  w0c, w1c, h_s, da_s, db_s, acc0, acc1, acco, back, send, recv, loc, p_send, p_recv):
+def expert_kernel(n_tp, n_ep, r_ref, d_ref, w0_ref, w1_ref, wo_ref, table_out, g0_out, g1_out, go_out, p0_out, p1_out, po_out, n0_out, n1_out, no_out,
+                  w0c, w1c, h_s, da_s, db_s, acc0, acc1, acco, back, send, recv, loc, p_send, p_recv, n_send, n_recv):
     s = lax.axis_index("tp")
     q = lax.axis_index("ep")
     me = s * n_ep + q
@@ -179,17 +179,24 @@
     acc1[...] = jnp.zeros_like(acc1)
     acco[...] = jnp.zeros_like(acco)
 
-    def row_copy(a, b):
+    step_rows = rows // 2
+
+    def row_copy(a, b, h):
         tp, ep = lax.rem(s + a, n_tp), lax.rem(q + b, n_ep)
-        return remote(back.at[tp, ep], table_out.at[me], send.at[a, b], recv.at[a, b], tp, ep)
-
-    own = pltpu.make_async_copy(back.at[s, q], table_out.at[me], loc)
-
-    def shard(i, _):
-        b = lax.rem(i + 1, n_ep)
+        sl = pl.ds(h * step_rows, step_rows)
+        return remote(back.at[tp, ep, sl], table_out.at[me, sl], send.at[h, a, b], recv.at[h, a, b], tp, ep)
+
+    def own(h):
+        sl = pl.ds(h * step_rows, step_rows)
+        return pltpu.make_async_copy(back.at[s, q, sl], table_out.at[me, sl], loc.at[h])
+
+    def half_shard(i, _):
+        h = lax.rem(i, 2)
+        b = lax.rem(i // 2 + 1, n_ep)
         ep = lax.rem(q + b, n_ep)
-        r = r_ref[ep]
-        d = d_ref[ep]
+        here = pl.ds(pl.multiple_of(h * step_rows, step_rows), step_rows)
+        r = r_ref[ep, here, :]
+        d = d_ref[ep, here, :]
         blk = 256
         for j in range(width // blk):
             sl = slice(j * blk, (j + 1) * blk)
@@ -206,29 +213,29 @@
             da_s[:, sl] = (dh * v * slope).astype(BF16)
         o = dot_nn(h_s[...], wo_ref[...]).astype(BF16).astype(F32)
         dr = (dot_nt(da_s[...], w0c[...]) + dot_nt(db_s[...], w1c[...])).astype(BF16).astype(F32)
-        low = lax.broadcasted_iota(jnp.int32, (rows, 128), 1) < 64
+        low = lax.broadcasted_iota(jnp.int32, (step_rows, 128), 1) < 64
         for j in range(d_model // 128):
             o_blk = o[:, j * 128:(j + 1) * 128]
             r_blk = dr[:, j * 128:(j + 1) * 128]
-            back[2 * j, ep] = jnp.where(low, o_blk, pltpu.roll(r_blk, 64, 1)).astype(BF16)
-            back[2 * j + 1, ep] = jnp.where(low, pltpu.roll(o_blk, 64, 1), r_blk).astype(BF16)
+            back[2 * j, ep, here, :] = jnp.where(low, o_blk, pltpu.roll(r_blk, 64, 1)).astype(BF16)
+            back[2 * j + 1, ep, here, :] = jnp.where(low, pltpu.roll(o_blk, 64, 1), r_blk).astype(BF16)
         for a in range(1, n_tp):
-            row_copy(a, b).start()
+            row_copy(a, b, h).start()
 
         @pl.when(b > 0)
         def _():
-            row_copy(0, b).start()
+            row_copy(0, b, h).start()
 
         @pl.when(b == 0)
         def _():
-            own.start()
+            own(h).start()
 
         acco[...] += dot_tn(h_s[...], d)
         acc0[...] += dot_tn(r, da_s[...])
         acc1[...] += dot_tn(r, db_s[...])
         return 0
 
-    lax.fori_loop(0, n_ep, shard, 0)
+    lax.fori_loop(0, 2 * n_ep, half_shard, 0)
     for j in range(n_tp):
         g0_out[j] = acc0[:, j * part:(j + 1) * part].astype(BF16)
         g1_out[j] = acc1[:, j * part:(j + 1) * part].astype(BF16)
@@ -240,17 +247,24 @@
         for k in range(n_tp // 2):
             crossing.append(remote(src.at[2 * k + 1 - y], dst.at[k], p_send.at[a, k], p_recv.at[a, k], s + 1 - 2 * y, q))
             crossing[-1].start()
-    own.wait()
-    for b in range(n_ep):
-        for a in range(n_tp):
-            if a + b > 0:
-                row_copy(a, b).wait()
+    z = s // 2
+    near = z + 1 - 2 * lax.rem(z, 2)
+    for a, (src, dst) in enumerate(((g0_out, n0_out), (g1_out, n1_out), (go_out, no_out))):
+        peer = 2 * near + y
+        crossing.append(remote(src.at[peer], dst, n_send.at[a], n_recv.at[a], peer, q))
+        crossing[-1].start()
+    for h in range(2):
+        own(h).wait()
+        for b in range(n_ep):
+            for a in range(n_tp):
+                if a + b > 0:
+                    row_copy(a, b, h).wait()
     for cp in crossing:
         cp.wait()
 
 
 def return_kernel(n_tp, n_ep, pos_ref, gcol_ref, dyc_ref, prob_ref, gate_ref, idx_ref, stat_ref, wgt_ref,
-                  table_ref, x_ref, g0_ref, g1_ref, go_ref, p0_ref, p1_ref, po_ref,
+                  table_ref, x_ref, g0_ref, g1_ref, go_ref, p0_ref, p1_ref, po_ref, n0_ref, n1_ref, no_ref,
                   gy_out, gx_out, g0_out, g1_out, go_out, dwg_out, aux_out,
                   tab_in, tab, c1, c2, y_buf, dr_buf, dg_buf, x_buf, tab_sem,
                   dg_all, dx_buf, dl_buf, dwg_buf, dwg_all,
@@ -266,14 +280,17 @@
     half = tokens // 2
     copies = []
     local = []
-    grads = ((g0_ref, p0_ref, g0_out), (g1_ref, p1_ref, g1_out), (go_ref, po_ref, go_out))
-    queue = [(a, h, p) for a in range(3) for p in range(1, n_z) for h in range(2)]
+    grads = ((g0_ref, p0_ref, n0_ref, g0_out), (g1_ref, p1_ref, n1_ref, g1_out), (go_ref, po_ref, no_ref, go_out))
+    queue = [(a, h, p) for a in range(3) for h, p in ((1, 1), (0, 1), (1, 2), (0, 2), (1, 3))]
+    near = z + 1 - 2 * lax.rem(z, 2)
 
     def send_grads(n):
         for _ in range(min(n, len(queue))):
             a, h, p = queue.pop(0)
-            own, other, dst = grads[a]
+            own, other, _, dst = grads[a]
             k = lax.rem(z + p, n_z)
+            if h == 0 and p == 1:
+                k = lax.rem(near + 2, n_z)
             src = other.at[k] if h else own.at[2 * k + y]
             source = s + 1 - 2 * y if h else s
             cp = remote(src, dst.at[source], g_send.at[a, h, p], g_recv.at[a, h, p], 2 * k + y, q)
@@ -281,11 +298,11 @@
             copies.append(cp)
 
     stay_in, stay_out = [], []
-    for a, (own, other, dst) in enumerate(grads):
-        for h, (src, source) in enumerate(((own.at[s], s), (other.at[z], s + 1 - 2 * y))):
+    for a, (own, other, close, dst) in enumerate(grads):
+        for h, (src, source) in enumerate(((own.at[s], s), (other.at[z], s + 1 - 2 * y), (close, 2 * near + y))):
             mid = stay_o.at[h] if a == 2 else stay_w.at[a, h]
             stay_in.append(pltpu.make_async_copy(src, mid, g_loc.at[a, h]))
-            stay_out.append(pltpu.make_async_copy(mid, dst.at[source], g_loc.at[a, 2 + h]))
+            stay_out.append(pltpu.make_async_copy(mid, dst.at[source], g_loc.at[a, 3 + h]))
     for cp in stay_in:
         cp.start()
 
@@ -399,7 +416,7 @@
         cp.start()
     x_load = pltpu.make_async_copy(x_ref, x_buf, loc.at[7])
     x_load.start()
-    send_grads(6)
+    send_grads(5)
 
     tab[pl.ds(slots, 8), :] = jnp.zeros((8, 128), F32)
     for k in range(groups):
@@ -522,9 +539,9 @@
     gat_y[1].relay(3)
     send_grads(3)
     gat_x[0].relay(2)
-    send_grads(3)
+    send_grads(2)
     gat_x[1].relay(2)
-    send_grads(3)
+    send_grads(2)
     gat_x[0].relay(3)
     gat_x[1].relay(3)
     send_grads(3)
@@ -600,18 +617,19 @@
         )(x_loc, dy_loc, idx_t, key_t, wgt, gelu_loc, lin_loc, out_loc)
 
         half_shape = lambda ref: sds((n_tp // 2,) + ref.shape[1:], BF16)
-        table, g0, g1, go, p0, p1, po = pl.pallas_call(
+        one_shape = lambda ref: sds(ref.shape[1:], BF16)
+        table, g0, g1, go, p0, p1, po, n0, n1, no = pl.pallas_call(
             functools.partial(expert_kernel, n_tp, n_ep),
             name="moe_expert",
             out_shape=(sds((n_tp * n_ep, cap, 128), BF16), sds(gelu_loc.shape, BF16), sds(lin_loc.shape, BF16), sds(out_loc.shape, BF16),
-                       half_shape(gelu_loc), half_shape(lin_loc), half_shape(out_loc)),
+                       half_shape(gelu_loc), half_shape(lin_loc), half_shape(out_loc), one_shape(gelu_loc), one_shape(lin_loc), one_shape(out_loc)),
             in_specs=[vmem] * 5,
-            out_specs=(hbm, vmem, vmem, vmem, hbm, hbm, hbm),
+            out_specs=(hbm, vmem, vmem, vmem) + (hbm,) * 6,
             scratch_shapes=[pltpu.VMEM((d_model, width), BF16), pltpu.VMEM((d_model, width), BF16),
-                            pltpu.VMEM((cap, width), BF16), pltpu.VMEM((cap, width), BF16), pltpu.VMEM((cap, width), BF16),
+                            pltpu.VMEM((cap // 2, width), BF16), pltpu.VMEM((cap // 2, width), BF16), pltpu.VMEM((cap // 2, width), BF16),
                             pltpu.VMEM((d_model, width), F32), pltpu.VMEM((d_model, width), F32), pltpu.VMEM((width, d_model), F32),
                             pltpu.VMEM((n_tp, n_ep, cap, 128), BF16),
-                            dma((n_tp, n_ep)), dma((n_tp, n_ep)), dma(()), dma((3, n_tp // 2)), dma((3, n_tp // 2))],
+                            dma((2, n_tp, n_ep)), dma((2, n_tp, n_ep)), dma((2,)), dma((3, n_tp // 2)), dma((3, n_tp // 2)), dma((3,)), dma((3,))],
             compiler_params=side,
         )(rows, drows, w0, w1, wo.reshape(width, d_model))
 
@@ -621,7 +639,7 @@
             out_shape=(sds((n_tp, tokens // 2, 128), BF16), sds((n_tp, tokens // 2, 128), BF16),
                        sds(gelu_loc.shape, BF16), sds(lin_loc.shape, BF16), sds(out_loc.shape, BF16),
                        sds((experts, d_model), F32), sds((1, 1), F32)),
-            in_specs=[pl.BlockSpec(memory_space=pltpu.SMEM)] + [vmem] * 7 + [hbm] * 8,
+            in_specs=[pl.BlockSpec(memory_space=pltpu.SMEM)] + [vmem] * 7 + [hbm] * 11,
             out_specs=(hbm, hbm, hbm, hbm, hbm, vmem, pl.BlockSpec(memory_space=pltpu.SMEM)),
             scratch_shapes=[pltpu.VMEM((n_tp * n_ep, cap, 128), BF16), pltpu.VMEM((slots + 8, 128), F32),
                             pltpu.VMEM((tokens, 128), F32), pltpu.VMEM((tokens, 128), F32),
@@ -629,11 +647,11 @@
                             pltpu.VMEM((tokens, d_model), BF16), dma((8,)),
                             pltpu.VMEM((n_tp, 8, tokens // 4), F32), pltpu.VMEM((tokens // 2, 128), BF16),
                             pltpu.VMEM((3 * experts, tokens), BF16), pltpu.VMEM((experts, d_model), F32), pltpu.VMEM((n_ep, experts, d_model), F32),
-                            pltpu.VMEM((2, 2, d_model, part), BF16), pltpu.VMEM((2, part, d_model), BF16),
-                            dma((3, 2, n_tp // 2)), dma((3, 2, n_tp // 2)), dma((3, 4)), dma((n_tp,)), dma((n_tp,)),
+                            pltpu.VMEM((2, 3, d_model, part), BF16), pltpu.VMEM((3, part, d_model), BF16),
+                            dma((3, 2, n_tp // 2)), dma((3, 2, n_tp // 2)), dma((3, 6)), dma((n_tp,)), dma((n_tp,)),
                             dma((4, n_tp, 3)), dma((4, n_tp)), dma((4,)), dma((n_ep,)), dma((n_ep,)), dma((8,))],
             compiler_params=side,
-        )(pos, gate_cols, dy_cols, prob, gate, idx_t, stat, wgt, table, x_loc, g0, g1, go, p0, p1, po)
+        )(pos, gate_cols, dy_cols, prob, gate, idx_t, stat, wgt, table, x_loc, g0, g1, go, p0, p1, po, n0, n1, no)
 
         pair = pl.BlockSpec((2, tokens // 2, 128), lambda j: (j, 0, 0))
         cols = pl.BlockSpec((tokens, 128), lambda j: (0, j))

time: 347 us -> 343 us (0.988)
  Pallas kernels: 342 us -> 337 us
    pallas_call x1, Pallas kernels: 149 us -> 142 us  [device_step(): pl.pallas_call(functools.partial(return_kernel, n_tp, n_ep), name='moe_re...]
where the time goes in v4:
time: 343 us
  Pallas kernels  337 us (98%)
    pallas_call x1, Pallas kernels, device_step(): pl.pallas_call(functools.partial(return_kernel, n_tp, n_ep), name='moe_re...  142 us
    pallas_call x1, Pallas kernels, device_step(): pl.pallas_call(functools.partial(expert_kernel, n_tp, n_ep), name='moe_ex...  112 us
    pallas_call x1, Pallas kernels, device_step(): pl.pallas_call(functools.partial(dispatch_kernel, n_tp, n_ep, cap), name=...  74.7 us
    pallas_call x1, Pallas kernels, device_step(): pl.pallas_call(interleave_kernel, name='moe_interleave', grid=(n_tp // 2,...  9.2 us

profile of v4, /device:TPU:0, one launch (start us, length us, event | category | flops | bytes accessed | tf_op | source)
XLA Modules:
  0.0 342.7 jit_solution(17800160728587519479)
XLA Ops:
  0.6 1.5 fusion.4
  2.2 0.6 copy.15
  2.8 74.7 %moe_dispatch.1 = (bf16[4,512,512]{2,1,0:T(8,128)(2,1)}, bf16[4,512,512]{2,1,0:T(8,128)(2,1)}, bf16[8,512,128]{2,1,0:T(8,128)(2,1)}, bf16[8,512,128]{2,1,0:T(8,1...) custom-call(bf16[4096,512]{1,0:T(8,128)(2,1)} %x_ref.3, ...), custom_call_target="tpu_custom_call" | custom-call | tf_op jit(solution)/shard_map/moe_dispatch/pallas_call | solution.py:603
  77.5 111.5 %moe_expert.1 = (bf16[32,512,128]{2,1,0:T(8,128)(2,1)}, bf16[8,512,128]{2,1,0:T(8,128)(2,1)}, bf16[8,512,128]{2,1,0:T(8,128)(2,1)}, bf16[8,128,512]{2,1,0:T(8,12...) custom-call(bf16[4,512,512]{2,1,0:T(8,128)(2,1)} %get-tuple-element., ...), custom_call_target="tpu_custom_call" | custom-call | tf_op jit(solution)/shard_map/moe_expert/pallas_call | solution.py:621
  189.0 142.1 %moe_return.1 = (bf16[8,2048,128]{2,1,0:T(8,128)(2,1)}, bf16[8,2048,128]{2,1,0:T(8,128)(2,1)}, bf16[8,512,128]{2,1,0:T(8,128)(2,1)}, bf16[8,512,128]{2,1,0:T(8,1...) custom-call(s32[8192]{0:T(1024)} %bitcast.29, f32[4096,8]{1,0:T(8,128)} %get-tuple-element.39.gcol_ref, ...), custom_call_target="tpu_custom_call" | custom-call | tf_op jit(solution)/shard_map/moe_return/pallas_call | solution.py:636
  331.1 0.0 copy-start
  331.1 9.2 %moe_interleave.1 = (bf16[4096,512]{1,0:T(8,128)(2,1)}, bf16[4096,512]{1,0:T(8,128)(2,1)}, bf16[8,512,128]{2,1,0:T(8,128)(2,1)}, bf16[8,512,128]{2,1,0:T(8,128)(2,1)}, bf16[8,128,512]{2,1,0:T(8,128)(2,1)}) custom-call(bf16[8,2048,128]{2,1,0:T(8,128)(2,1)} %get-tuple-element.59.gy_ref, bf16[8,2048,128]{2,1,0:T(8,128)(2,1)} %get-tuple-element.60.gx_ref, ...), custom_call_target="tpu_custom_call" | custom-call | tf_op jit(solution)/shard_map/moe_interleave/pallas_call | solution.py:659
  340.3 0.0 copy-done
  340.3 0.6 copy.18
Async XLA Ops:
  331.1 9.2 %copy-start = (f32[32,512]{1,0:T(8,128)S(1)}, f32[32,512]{1,0:T(8,128)}, u32[]{:S(2)}) copy-start(f32[32,512]{1,0:T(8,128)} %get-tuple-element.69) | copy-start | bytes 196612
